TPU v7x, 32 devices: a whole 2x2x4 slice. The times are simulated.
32 devices in a mesh: dom: 8 (over z, y), col: 2 (over x), batch: 2 (over core).
Axes of the slice: x: 2, y: 2, z: 4, core: 2. Of those that a mesh axis runs over, the one named last changes fastest.
Arguments:
- features: bfloat16 [16384, 128], P('dom', 'col'), may hold values from -6 to 6
- self_weight1: bfloat16 [128, 256], P('col', 'batch'), may hold values from -0.5 to 0.5
- neigh_weight1: bfloat16 [128, 256], P('col', 'batch'), may hold values from -2 to 2
- need_first: int32 [16, 64], P(('dom', 'batch')), may hold values from 0 to 127, as said below
- count_first: int32 [16], P(('dom', 'batch')), may hold values from 0 to 64
- adjacency_first: int32 [16384, 512], P(('dom', 'batch')), may hold values from 0 to 16384, as said below
- self_weight2: bfloat16 [256, 172], P('col', 'batch'), may hold values from -0.375 to 0.375
- neigh_weight2: bfloat16 [256, 172], P('col', 'batch'), may hold values from -0.375 to 0.375
- need_second: int32 [16, 64], P(('dom', 'batch')), may hold values from 0 to 127, as said below
- count_second: int32 [16], P(('dom', 'batch')), may hold values from 0 to 64
- adjacency_second: int32 [16384, 512], P(('dom', 'batch')), may hold values from 0 to 16384, as said below
- seed_rows: int32 [16384], P(('dom', 'batch')), may hold values from 0 to 2047
Outputs:
- logits: float32 [16384, 172], P(('dom', 'batch'))
Inputs may be any that keep to these rules, and one draw needn't show every extreme that they name: `need_first`: each row lists 64 different node blocks in increasing order; block g holds nodes 128 * g to 128 * g + 127 and lies in partition g // 16. At most 16 entries of one row lie in one partition, and exactly 16 lie in some partition in every row. `need_second`: each row lists 64 different frontier blocks in increasing order; block g holds frontier rows 128 * g to 128 * g + 127 and lies in partition g // 16. At most 16 entries of one row lie in one partition, and exactly 16 lie in some partition in every row. `adjacency_first`: bit i of word k of a row is the adjacency entry of column 16 k + i; at most one bit of a word is set, and bit 15 never. `adjacency_second`: bit i of word k of a row is the adjacency entry of column 16 k + i; at most one bit of a word is set, and bit 15 never.
All inputs are finite; a program needn't handle non-finite values.
Results may differ from a plain program's by a relative error of at most 0.0036.
Values may be sent and summed in bfloat16 or wider, within the bound.
No kernel may reach another device: no remote copies, remote signals or barrier semaphores. Data moves between devices by JAX's collectives and lax.ppermute only.
A program may use at most 128 MiB of HBM per device.

v0:
```python
import functools

import jax
import jax.numpy as jnp
from jax import lax
from jax.experimental import pallas as pl
from jax.experimental.pallas import tpu as pltpu
from jax.sharding import PartitionSpec as P


BLK = 128
BITS = 16
PLANES = 15
WORDS = BLK // BITS
LANES = 128
MESH_AXES = ("dom", "col", "batch")
VMEM = pl.BlockSpec(memory_space=pltpu.VMEM)
SMEM = pl.BlockSpec(memory_space=pltpu.SMEM)
ANY = pl.BlockSpec(memory_space=pl.ANY)
PARAMS = pltpu.CompilerParams(vmem_limit_bytes=36 * 2**20)


def lanes_for(width):
    need = max((PLANES - 1) * width + LANES, BITS * width if width % 64 == 0 else 0)
    return -(-need // LANES) * LANES


def shift_perm(sizes, which, by):
    pairs = []
    total = 1
    for size in sizes:
        total *= size
    for source in range(total):
        place = []
        rest = source
        for size in reversed(sizes):
            place.append(rest % size)
            rest //= size
        place = place[::-1]
        place[which] = (place[which] + by) % sizes[which]
        target = 0
        for size, at in zip(sizes, place):
            target = target * size + at
        pairs.append((source, target))
    return pairs


def pack_planes(tall_ref, out_ref, width, planes):
    words = out_ref.shape[0]
    for i in range(planes):
        piece = tall_ref[pl.ds(i, words, stride=BITS), :]
        out_ref[:, i * width : (i + 1) * width] = piece[:, :width]


def fetch_words(adj_ref, words_ref, sem):
    rows = adj_ref.shape[0] // sem.shape[0]
    copies = [
        pltpu.make_async_copy(adj_ref.at[pl.ds(n * rows, rows)], words_ref.at[pl.ds(n * rows, rows)], sem.at[n])
        for n in range(sem.shape[0])
    ]
    for copy in copies:
        copy.start()
    return copies


def pick_blocks(low_ref, high_ref, local_ref, pieces, picked_ref):
    for n, piece in enumerate(pieces):

        def pick(b, _, piece=piece):
            at = pl.multiple_of(b * WORDS, WORDS)
            picked_ref[pl.ds(at, WORDS), :] = piece[local_ref[b]].astype(jnp.float32)
            return 0

        lax.fori_loop(low_ref[n], high_ref[n], pick, 0)


def mean_rows(count, words_ref, copies, short_ref, picked_ref, total_ref, width):
    rows = words_ref.shape[0] // len(copies)
    degrees = []
    for n, copy in enumerate(copies):
        copy.wait()
        words = words_ref[n * rows : (n + 1) * rows, :]
        column = lax.broadcasted_iota(jnp.int32, words.shape, 1)
        words = jnp.where(column < count * WORDS, words, 0)
        degrees.append(jnp.sum(jnp.where(words != 0, 1.0, 0.0), axis=1, keepdims=True))
        short_ref[n * rows : (n + 1) * rows, :] = words.astype(jnp.int16)
    short = short_ref.shape
    one, zero = jnp.ones(short, jnp.bfloat16), jnp.zeros(short, jnp.bfloat16)
    for i in range(PLANES):
        table = picked_ref[:, i * width : i * width + LANES].astype(jnp.bfloat16)
        mask = jnp.where(short_ref[...] == jnp.int16(1 << i), one, zero)
        part = jnp.dot(mask, table, preferred_element_type=jnp.float32)
        if i == 0:
            total_ref[...] = part
        else:
            total_ref[...] += part
    return total_ref[...] / jnp.maximum(jnp.concatenate(degrees, axis=0), 1.0)


def mean_first_kernel(width, n_pieces, low_ref, high_ref, local_ref, count_ref, adj_ref, *rest):
    pieces, out_ref = rest[:n_pieces], rest[n_pieces]
    words_ref, short_ref, picked_ref, total_ref, sem, wide_ref = rest[n_pieces + 1 :]
    copies = fetch_words(adj_ref, words_ref, sem)
    pick_blocks(low_ref, high_ref, local_ref, pieces, picked_ref)
    total_ref[...] = mean_rows(count_ref[0], words_ref, copies, short_ref, picked_ref, total_ref, width)
    pack_planes(total_ref, wide_ref, width, BITS)
    out_ref[...] = wide_ref[...].astype(jnp.bfloat16)


def mean_second_kernel(width, n_pieces, low_ref, high_ref, local_ref, count_ref, adj_ref, *rest):
    pieces, (own_ref, out_ref) = rest[:n_pieces], rest[n_pieces : n_pieces + 2]
    words_ref, short_ref, picked_ref, total_ref, sem = rest[n_pieces + 2 :]
    copies = fetch_words(adj_ref, words_ref, sem)
    pick_blocks(low_ref, high_ref, local_ref, pieces, picked_ref)
    mean = mean_rows(count_ref[0], words_ref, copies, short_ref, picked_ref, total_ref, width)
    out_ref[...] = (mean.T[:width, :] + own_ref[...]).astype(jnp.bfloat16)


def here(array):
    return pltpu.with_memory_space_constraint(array, pltpu.VMEM)


def mean_call(kernel, lists, count, adjacency, pieces, more, out_shape, extra, width):
    rows, row_words = adjacency.shape
    lanes = pieces[0].shape[2]
    return pl.pallas_call(
        functools.partial(kernel, width, len(pieces)),
        in_specs=[SMEM] * 4 + [ANY] + [VMEM] * (len(pieces) + len(more)),
        out_specs=VMEM,
        out_shape=out_shape,
        scratch_shapes=[
            pltpu.VMEM((rows, row_words), jnp.int32),
            pltpu.VMEM((rows, row_words), jnp.int16),
            pltpu.VMEM((row_words, lanes), jnp.float32),
            pltpu.VMEM((rows, LANES), jnp.float32),
            pltpu.SemaphoreType.DMA((4,)),
        ]
        + extra,
        compiler_params=PARAMS,
        cost_estimate=pl.CostEstimate(
            flops=2 * rows * row_words * PLANES * LANES, bytes_accessed=4 * rows * row_words, transcendentals=0
        ),
    )(*lists, count, adjacency, *[here(p) for p in pieces], *[here(m) for m in more])


def hidden_kernel(width, classes, self_own, self_far, near_own, near_far, weight_ref, out_weight_ref, hidden_ref, wide_ref, rows_ref, tall_ref, scratch_ref):
    words = self_own.shape[0]
    parts = (self_own, self_far, near_own, near_far)
    for i in range(BITS):
        for n, part in enumerate(parts):
            rows_ref[pl.ds(i * words, words), n * width : (n + 1) * width] = part[:, i * width : (i + 1) * width]
    hidden = jnp.dot(rows_ref[...], weight_ref[...], preferred_element_type=jnp.float32)
    hidden = jnp.maximum(hidden, 0.0).astype(jnp.bfloat16)
    hidden_ref[...] = hidden
    tall_ref[...] = jnp.dot(hidden, out_weight_ref[...], preferred_element_type=jnp.float32)
    scratch_ref[...] = jnp.zeros_like(scratch_ref)
    for i in range(PLANES):
        scratch_ref[:, i * classes : (i + 1) * classes] = tall_ref[pl.ds(i * words, words), :classes]
    wide_ref[...] = scratch_ref[...].astype(jnp.bfloat16)


def own_kernel(seed_ref, weight_ref, *rest):
    hidden_refs, out_ref = rest[:-1], rest[-1]
    total = jnp.zeros(out_ref.shape, jnp.float32)
    for n, hidden_ref in enumerate(hidden_refs):
        rows = hidden_ref.shape[0]
        every = lax.dot_general(
            weight_ref[...], hidden_ref[...], (((1,), (1,)), ((), ())), preferred_element_type=jnp.float32
        )
        high = every.astype(jnp.bfloat16)
        low = (every - high.astype(jnp.float32)).astype(jnp.bfloat16)
        place = lax.broadcasted_iota(jnp.int32, (rows, seed_ref.shape[1]), 0) + n * rows
        chosen = jnp.where(place == seed_ref[...], 1.0, 0.0).astype(jnp.bfloat16)
        total += jnp.dot(high, chosen, preferred_element_type=jnp.float32)
        total += jnp.dot(low, chosen, preferred_element_type=jnp.float32)
    out_ref[...] = total


def per_device(
    grid,
    features,
    self_weight1,
    neigh_weight1,
    need_first,
    count_first,
    adjacency_first,
    self_weight2,
    neigh_weight2,
    need_second,
    count_second,
    adjacency_second,
    seed_rows,
):
    outer, inner, n_col, n_batch = grid
    dom_at, col_at, batch_at = (lax.axis_index(a) for a in MESH_AXES)

    def move(array, which, by):
        return lax.ppermute(array, MESH_AXES, shift_perm(grid, which, by))

    def ring(array, which):
        return [array] + [move(array, which, by) for by in range(1, grid[which])]

    def gather_blocks(piece):
        return [last for first in ring(piece, 0) for second in ring(first, 1) for last in ring(second, 3)]

    def in_order(relative, at):
        n = len(relative)
        ordered = []
        for owner in range(n):
            chosen = relative[0]
            for back in range(1, n):
                chosen = jnp.where((at - owner) % n == back, relative[back], chosen)
            ordered.append(chosen)
        return ordered

    width = features.shape[1]
    rows = adjacency_first.shape[0]
    words = rows // BITS
    lanes = lanes_for(width)
    blocks = rows // BLK

    piece_owner = jnp.stack(
        [
            (((dom_at // inner - ko) % outer) * inner + (dom_at - ki) % inner) * n_batch + (batch_at - kb) % n_batch
            for ko in range(outer)
            for ki in range(inner)
            for kb in range(n_batch)
        ]
    )

    def lists(wanted):
        holder = wanted // blocks
        low = jnp.sum((holder[None, :] < piece_owner[:, None]).astype(jnp.int32), axis=1)
        high = jnp.sum((holder[None, :] <= piece_owner[:, None]).astype(jnp.int32), axis=1)
        return low, high, wanted % blocks

    own = lax.dynamic_slice_in_dim(features, batch_at * rows, rows, 0).reshape(words, BITS * width)
    if lanes > BITS * width:
        own = jnp.pad(own, ((0, 0), (0, lanes - BITS * width)))
    pieces_first = gather_blocks(own.reshape(blocks, WORDS, lanes))

    self_parts = ring(own, 2)
    class_cols = self_weight2.shape[1]
    packed = jnp.concatenate([self_weight1, neigh_weight1, self_weight2.T, neigh_weight2.T], axis=0)
    packs = [in_order(ring(a, 3), batch_at) for a in ring(packed, 2)]
    full = [jnp.concatenate([a[: 2 * width] for a in row], axis=1) for row in packs]
    weight_first = jnp.concatenate([f[:width] for f in full] + [f[width:] for f in full], axis=0)
    rows2 = [[a[2 * width :] for a in row] for row in packs]
    classes = class_cols * n_batch // n_col

    def class_rows(low):
        whole = jnp.concatenate(
            in_order([jnp.concatenate([a[low : low + class_cols] for a in row], axis=0) for row in rows2], col_at),
            axis=1,
        )
        return lax.dynamic_slice_in_dim(whole, col_at * classes, classes, 0)

    weight_own = class_rows(0)
    weight_far = jnp.pad(class_rows(class_cols).T, ((0, 0), (0, LANES - classes)))

    near = mean_call(
        mean_first_kernel,
        lists(need_first[0]),
        count_first,
        adjacency_first,
        pieces_first,
        [],
        pltpu.VMEM((words, lanes), jnp.bfloat16),
        [pltpu.VMEM((words, lanes), jnp.float32)],
        width,
    )
    near_parts = ring(near, 2)
    wide = lanes_for(classes)
    hidden, scores = pl.pallas_call(
        functools.partial(hidden_kernel, width, classes),
        in_specs=[VMEM] * 6,
        out_specs=[VMEM] * 2,
        out_shape=[
            pltpu.VMEM((rows, weight_first.shape[1]), jnp.bfloat16),
            pltpu.VMEM((words, wide), jnp.bfloat16),
        ],
        scratch_shapes=[
            pltpu.VMEM((rows, weight_first.shape[0]), jnp.bfloat16),
            pltpu.VMEM((rows, LANES), jnp.float32),
            pltpu.VMEM((words, wide), jnp.float32),
        ],
        compiler_params=PARAMS,
        name="hidden",
    )(*[here(a) for a in (*self_parts, *near_parts, weight_first, weight_far)])

    pieces_second = gather_blocks(scores.reshape(blocks, WORDS, wide))
    inside = seed_rows % rows
    place = ((batch_at - seed_rows // rows) % n_batch) * rows + (inside % BITS) * words + inside // BITS
    seeds = seed_rows.shape[0]
    own_call = pl.pallas_call(
        own_kernel,
        in_specs=[VMEM] * (2 + n_batch),
        out_specs=VMEM,
        out_shape=pltpu.VMEM((classes, seeds), jnp.float32),
        compiler_params=PARAMS,
        cost_estimate=pl.CostEstimate(
            flops=12 * rows * n_batch * seeds * LANES, bytes_accessed=4 * classes * seeds, transcendentals=0
        ),
        name="own_rows",
    )
    hidden_parts = ring(hidden, 3)
    own_second = own_call(place.reshape(1, seeds), weight_own, *[here(h) for h in hidden_parts])
    half = mean_call(
        mean_second_kernel,
        lists(need_second[0]),
        count_second,
        adjacency_second,
        pieces_second,
        [own_second],
        pltpu.VMEM((classes, seeds), jnp.bfloat16),
        [],
        classes,
    )
    logits = jnp.concatenate(in_order(ring(half, 2), col_at), axis=0)
    return logits.astype(jnp.float32).T


def solution(mesh):
    sizes = tuple(mesh.shape[a] for a in MESH_AXES)
    inner = 2 if sizes[0] % 2 == 0 else 1
    grid = (sizes[0] // inner, inner, sizes[1], sizes[2])
    placed = (
        P("dom", "col"),
        P("col", "batch"),
        P("col", "batch"),
        P(("dom", "batch"), None),
        P(("dom", "batch")),
        P(("dom", "batch"), None),
        P("col", "batch"),
        P("col", "batch"),
        P(("dom", "batch"), None),
        P(("dom", "batch")),
        P(("dom", "batch"), None),
        P(("dom", "batch")),
    )

    def body(*args):
        return per_device(grid, *args)

    return jax.shard_map(
        body, mesh=mesh, in_specs=placed, out_specs=P(("dom", "batch"), None), check_vma=False
    )
```

profile of v0, /device:TPU:24, one launch (start us, length us, event | category | flops | bytes accessed | tf_op | source)
XLA Modules:
  0.0 90.9 jit_solution(2429585534249318558)
XLA Ops:
  0.0 1.6 %pad_maximum_fusion = bf16[300,128]{1,0:T(8,128)(2,1)} fusion(bf16[86,128]{1,0:T(8,128)(2,1)} %bitcast.39, bf16[86,128]{1,0:T(8,128)(2,1)} %bitcast.41, bf16[64,128]{1,0:T(8,128)(2,1)} %param.14, bf16[64,128]{1,0:T(8,128)(2,1)} %param.13), kind=kLoop, calls=%fused_computation.19 | loop fusion | flops 307200 | bytes 153600 | tf_op jit(solution)/shard_map/concatenate | solution.py:244
  1.6 1.5 %collective-permute-start.18 = (bf16[300,128]{1,0:T(8,128)(2,1)}, bf16[300,128]{1,0:T(8,128)(2,1)S(1)}, u32[]{:S(2)}, u32[]{:S(2)}) collective-permute-start(bf16[300,128]{1,0:T(8,128)(2,1)} %pad_maximum_fusion), channel_id=1, source_target_pairs={{0,2},{1,3},{2,0},{3,1},{4,6},{5,7},{6,4},{7,5},{8,10},{9,11},{10,... | collective-permute-start | bytes 230408 | tf_op jit(solution)/shard_map/ppermute | solution.py:198
  3.1 0.0 collective-permute-start.17
  3.1 0.2 copy.19
  3.3 0.2 reshape_reshape.3.rest_0_
  3.5 0.4 collective-permute-start.8
  3.9 0.4 collective-permute-start.12
  4.3 3.4 %collective-permute-start.4 = (bf16[8,8,1024]{2,1,0:T(8,128)(2,1)S(1)}, bf16[8,8,1024]{2,1,0:T(8,128)(2,1)S(1)}, u32[]{:S(2)}, u32[]{:S(2)}) collective-permute-start(bf16[8,8,1024]{2,1,0:T(8,128)(2,1)S(1)} %reshape_reshape.3.rest_0_), channel_id=1, source_target_pairs={{0,8},{1,9},{2,10},{3,11},{4,12},{5,13},{6,14},{7,15},{8,16},{9,17... | collective-permute-start | bytes 393224 | tf_op jit(solution)/shard_map/ppermute | solution.py:198
  7.7 0.2 reshape.10.self_own
  7.9 0.7 and_select_fusion.local_ref
  8.6 0.7 fusion.27
  9.9 0.1 stack.67
  10.0 0.2 convert_reduce_fusion
  10.2 0.0 collective-permute-done.18
  10.2 1.6 %collective-permute-start.2 = (bf16[8,8,1024]{2,1,0:T(8,128)(2,1)S(1)}, bf16[8,8,1024]{2,1,0:T(8,128)(2,1)S(1)}, u32[]{:S(2)}, u32[]{:S(2)}) collective-permute-start(bf16[8,8,1024]{2,1,0:T(8,128)(2,1)S(1)} %reshape_reshape.3.rest_0_), channel_id=1, source_target_pairs={{0,4},{1,5},{2,6},{3,7},{4,0},{5,1},{6,2},{7,3},{8,12},{9,13},{10,... | collective-permute-start | bytes 393224 | tf_op jit(solution)/shard_map/ppermute | solution.py:198
  11.8 0.0 collective-permute-start.19
  11.8 0.8 broadcast_select_fusion.5
  12.7 0.9 collective-permute-done.12.rest_12_
  13.6 1.5 %collective-permute-start.14 = (bf16[8,8,1024]{2,1,0:T(8,128)(2,1)S(1)}, bf16[8,8,1024]{2,1,0:T(8,128)(2,1)S(1)}, u32[]{:S(2)}, u32[]{:S(2)}) collective-permute-start(bf16[8,8,1024]{2,1,0:T(8,128)(2,1)S(1)} %collective-permute-done.12.rest_12_), channel_id=1, source_target_pairs={{0,4},{1,5},{2,6},{3,7},{4,0},{5,1},{6,2},{7,3},{8,12},{9,13},{10,... | collective-permute-start | bytes 393224 | tf_op jit(solution)/shard_map/ppermute | solution.py:198
  15.2 0.8 collective-permute-done.8.rest_8_
  15.9 0.0 collective-permute-start.13
  16.0 0.3 collective-permute-done.4.rest_4_
  16.2 1.5 %collective-permute-start.6 = (bf16[8,8,1024]{2,1,0:T(8,128)(2,1)S(1)}, bf16[8,8,1024]{2,1,0:T(8,128)(2,1)S(1)}, u32[]{:S(2)}, u32[]{:S(2)}) collective-permute-start(bf16[8,8,1024]{2,1,0:T(8,128)(2,1)S(1)} %collective-permute-done.4.rest_4_), channel_id=1, source_target_pairs={{0,4},{1,5},{2,6},{3,7},{4,0},{5,1},{6,2},{7,3},{8,12},{9,13},{10,... | collective-permute-start | bytes 393224 | tf_op jit(solution)/shard_map/ppermute | solution.py:198
  17.7 0.6 collective-permute-start.10
  18.3 0.6 fusion.29
  18.9 6.2 %collective-permute-done.10.rest_10_ = bf16[8,8,1024]{2,1,0:T(8,128)(2,1)S(1)} collective-permute-done((bf16[8,8,1024]{2,1,0:T(8,128)(2,1)S(1)}, bf16[8,8,1024]{2,1,0:T(8,128)(2,1)S(1)}, u32[]{:S(2)}, u32[]{:S(2)}) %collective-permute-start.10) | collective-permute-done | bytes 131104 | tf_op jit(solution)/shard_map/ppermute | solution.py:198
  25.1 0.0 collective-permute-done.14.rest_14_
  25.1 0.5 collective-permute-start.3
  25.6 0.0 collective-permute-done.6.rest_6_
  25.6 0.1 collective-permute-start.11
  25.7 0.4 collective-permute-start.15
  26.2 0.0 collective-permute-done.5.rest_5_
  26.2 0.1 collective-permute-start.7
  26.3 0.2 collective-permute-done.9.rest_9_
  26.5 0.5 collective-permute-start
  27.0 0.0 collective-permute-done.3.rest_3_
  27.0 0.2 collective-permute-done.15.rest_15_
  27.2 0.3 collective-permute-done.7.rest_7_
  27.5 6.2 %shard_map.118.near_own = bf16[64,1024]{1,0:T(8,128)(2,1)S(1)} custom-call(s32[16]{0:T(128)S(1)} %get-tuple-element.10.low_ref, s32[16]{0:T(128)S(1)} %get-tuple-element.9.high_ref, s32[64]{0:T(128)S(1)} %and_select_fusion.local_ref, s32[1]{0:T(128)S(6)} %copy.23.count_ref, s32[1024,512]{1,0:T(8,128)S(1)} %copy-done.1, ...), custom_call_target="tpu_custom_call" | custom-call | flops 2013265920 | bytes 2097152 | tf_op jit(solution)/shard_map/pallas_call | solution.py:126
  33.8 1.1 %collective-permute-start.16 = (bf16[64,1024]{1,0:T(8,128)(2,1)S(1)}, bf16[64,1024]{1,0:T(8,128)(2,1)S(1)}, u32[]{:S(2)}, u32[]{:S(2)}) collective-permute-start(bf16[64,1024]{1,0:T(8,128)(2,1)S(1)} %shard_map.118.near_own), channel_id=1, source_target_pairs={{0,2},{1,3},{2,0},{3,1},{4,6},{5,7},{6,4},{7,5},{8,10},{9,11},{10,... | collective-permute-start | bytes 393224 | tf_op jit(solution)/shard_map/ppermute | solution.py:198
  34.9 0.1 copy.22
  35.1 4.3 %collective-permute-done.16.near_far = bf16[64,1024]{1,0:T(8,128)(2,1)S(1)} collective-permute-done((bf16[64,1024]{1,0:T(8,128)(2,1)S(1)}, bf16[64,1024]{1,0:T(8,128)(2,1)S(1)}, u32[]{:S(2)}, u32[]{:S(2)}) %collective-permute-start.16) | collective-permute-done | bytes 131104 | tf_op jit(solution)/shard_map/ppermute | solution.py:198
  39.4 0.8 hidden.1
  40.2 0.1 collective-permute-start.23
  40.3 4.6 %collective-permute-start.27 = (bf16[8,8,1408]{2,1,0:T(8,128)(2,1)S(1)}, bf16[8,8,1408]{2,1,0:T(8,128)(2,1)S(1)}, u32[]{:S(2)}, u32[]{:S(2)}) collective-permute-start(bf16[8,8,1408]{2,1,0:T(8,128)(2,1)S(1)} %bitcast.34), channel_id=1, source_target_pairs={{0,16},{1,17},{2,18},{3,19},{4,20},{5,21},{6,22},{7,23},{8,24},{9,... | collective-permute-start | bytes 540680 | tf_op jit(solution)/shard_map/ppermute | solution.py:198
  45.5 2.0 %collective-permute-start.31 = (bf16[8,8,1408]{2,1,0:T(8,128)(2,1)S(1)}, bf16[8,8,1408]{2,1,0:T(8,128)(2,1)S(1)}, u32[]{:S(2)}, u32[]{:S(2)}) collective-permute-start(bf16[8,8,1408]{2,1,0:T(8,128)(2,1)S(1)} %bitcast.35), channel_id=1, source_target_pairs={{0,24},{1,25},{2,26},{3,27},{4,28},{5,29},{6,30},{7,31},{8,0},{9,1... | collective-permute-start | bytes 540680 | tf_op jit(solution)/shard_map/ppermute | solution.py:198
  47.5 1.5 %collective-permute-start.21 = (bf16[8,8,1408]{2,1,0:T(8,128)(2,1)S(1)}, bf16[8,8,1408]{2,1,0:T(8,128)(2,1)S(1)}, u32[]{:S(2)}, u32[]{:S(2)}) collective-permute-start(bf16[8,8,1408]{2,1,0:T(8,128)(2,1)S(1)} %bitcast.36), channel_id=1, source_target_pairs={{0,4},{1,5},{2,6},{3,7},{4,0},{5,1},{6,2},{7,3},{8,12},{9,13},{10,... | collective-permute-start | bytes 540680 | tf_op jit(solution)/shard_map/ppermute | solution.py:198
  49.0 11.3 %collective-permute-done.27.rest_8_ = bf16[8,8,1408]{2,1,0:T(8,128)(2,1)S(1)} collective-permute-done((bf16[8,8,1408]{2,1,0:T(8,128)(2,1)S(1)}, bf16[8,8,1408]{2,1,0:T(8,128)(2,1)S(1)}, u32[]{:S(2)}, u32[]{:S(2)}) %collective-permute-start.27) | collective-permute-done | bytes 180256 | tf_op jit(solution)/shard_map/ppermute | solution.py:198
  60.4 1.5 %collective-permute-start.25 = (bf16[8,8,1408]{2,1,0:T(8,128)(2,1)S(1)}, bf16[8,8,1408]{2,1,0:T(8,128)(2,1)S(1)}, u32[]{:S(2)}, u32[]{:S(2)}) collective-permute-start(bf16[8,8,1408]{2,1,0:T(8,128)(2,1)S(1)} %collective-permute-done.23.rest_4_), channel_id=1, source_target_pairs={{0,4},{1,5},{2,6},{3,7},{4,0},{5,1},{6,2},{7,3},{8,12},{9,13},{10,... | collective-permute-start | bytes 540680 | tf_op jit(solution)/shard_map/ppermute | solution.py:198
  61.9 0.1 collective-permute-start.24
  62.0 0.6 collective-permute-start.29
  62.6 1.5 %collective-permute-start.33 = (bf16[8,8,1408]{2,1,0:T(8,128)(2,1)S(1)}, bf16[8,8,1408]{2,1,0:T(8,128)(2,1)S(1)}, u32[]{:S(2)}, u32[]{:S(2)}) collective-permute-start(bf16[8,8,1408]{2,1,0:T(8,128)(2,1)S(1)} %collective-permute-done.31.rest_12_), channel_id=1, source_target_pairs={{0,4},{1,5},{2,6},{3,7},{4,0},{5,1},{6,2},{7,3},{8,12},{9,13},{10,... | collective-permute-start | bytes 540680 | tf_op jit(solution)/shard_map/ppermute | solution.py:198
  64.1 2.6 %collective-permute-done.25.rest_6_ = bf16[8,8,1408]{2,1,0:T(8,128)(2,1)S(1)} collective-permute-done((bf16[8,8,1408]{2,1,0:T(8,128)(2,1)S(1)}, bf16[8,8,1408]{2,1,0:T(8,128)(2,1)S(1)}, u32[]{:S(2)}, u32[]{:S(2)}) %collective-permute-start.25) | collective-permute-done | bytes 180256 | tf_op jit(solution)/shard_map/ppermute | solution.py:198
  66.7 0.8 broadcast_select_fusion.6
  67.6 3.0 %collective-permute-done.29.rest_10_ = bf16[8,8,1408]{2,1,0:T(8,128)(2,1)S(1)} collective-permute-done((bf16[8,8,1408]{2,1,0:T(8,128)(2,1)S(1)}, bf16[8,8,1408]{2,1,0:T(8,128)(2,1)S(1)}, u32[]{:S(2)}, u32[]{:S(2)}) %collective-permute-start.29) | collective-permute-done | bytes 180256 | tf_op jit(solution)/shard_map/ppermute | solution.py:198
  70.6 3.0 %collective-permute-done.33.rest_14_ = bf16[8,8,1408]{2,1,0:T(8,128)(2,1)S(1)} collective-permute-done((bf16[8,8,1408]{2,1,0:T(8,128)(2,1)S(1)}, bf16[8,8,1408]{2,1,0:T(8,128)(2,1)S(1)}, u32[]{:S(2)}, u32[]{:S(2)}) %collective-permute-start.33) | collective-permute-done | bytes 180256 | tf_op jit(solution)/shard_map/ppermute | solution.py:198
  73.6 0.5 collective-permute-start.26
  74.1 0.1 collective-permute-start.30
  74.2 0.4 collective-permute-start.34
  74.6 2.2 %own_rows.1.rest_16_ = f32[86,1024]{1,0:T(8,128)S(1)} custom-call(s32[1,1024]{1,0:T(1,128)S(1)} %bitcast.32, bf16[86,256]{1,0:T(8,128)(2,1)S(1)} %fusion.9.weight_ref, bf16[1024,256]{1,0:T(8,128)(2,1)S(1)} %get-tuple-element.8.rest_0_, bf16[1024,256]{1,0:T(8,128)(2,1)S(1)} %collective-permute-done.35.rest_1_), custom_call_target="tpu_custom_call" | custom-call | flops 3221225472 | bytes 352256 | tf_op jit(solution)/shard_map/own_rows/pallas_call | solution.py:307
  76.9 6.4 %shard_map.119 = bf16[86,1024]{1,0:T(8,128)(2,1)S(1)} custom-call(s32[16]{0:T(128)S(1)} %get-tuple-element.13.low_ref, s32[16]{0:T(128)S(1)} %get-tuple-element.14.high_ref, s32[64]{0:T(128)S(1)} %and_select_fusion.2.local_ref, s32[1]{0:T(128)S(6)} %copy.24.count_ref, s32[1024,512]{1,0:T(8,128)S(1)} %copy-done.2, bf16[8,8,1408]{2,1,0:T(8,128)(2,1)S(1)} %bitcast.38, ...), custom_call_target="tpu_custom_call" | custom-call | flops 2013265920 | bytes 2097152 | tf_op jit(solution)/shard_map/pallas_call | solution.py:126
  83.4 0.8 collective-permute-start.36
  84.2 5.7 %collective-permute-done.36 = bf16[86,1024]{1,0:T(8,128)(2,1)S(1)} collective-permute-done((bf16[86,1024]{1,0:T(8,128)(2,1)S(1)}, bf16[86,1024]{1,0:T(8,128)(2,1)S(1)}, u32[]{:S(2)}, u32[]{:S(2)}) %collective-permute-start.36) | collective-permute-done | bytes 176160 | tf_op jit(solution)/shard_map/ppermute | solution.py:198
  90.0 0.9 %convert_bitcast_fusion = f32[1024,172]{0,1:T(8,128)} fusion(bf16[86,1024]{1,0:T(8,128)(2,1)S(1)} %get-tuple-element.16, bf16[86,1024]{1,0:T(8,128)(2,1)S(1)} %get-tuple-element.15), kind=kLoop, calls=%fused_computation | loop fusion | flops 704512 | bytes 1056768 | tf_op jit(solution)/shard_map/transpose | solution.py:320
  (53 shorter events, 0.3 us)
Async XLA Ops:
  0.0 3.1 %copy-start = (bf16[2048,64]{0,1:T(8,128)(2,1)S(1)}, bf16[2048,64]{0,1:T(8,128)(2,1)}, u32[]{:S(2)}) copy-start(bf16[2048,64]{0,1:T(8,128)(2,1)} %param.12) | copy-start | bytes 786436
  0.0 27.5 %copy-start.1 = (s32[1024,512]{1,0:T(8,128)S(1)}, s32[1024,512]{1,0:T(8,128)}, u32[]{:S(2)}) copy-start(s32[1024,512]{1,0:T(8,128)} %adj_ref.2) | copy-start | bytes 6291460
  1.6 8.7 %collective-permute-start.18 = (bf16[300,128]{1,0:T(8,128)(2,1)}, bf16[300,128]{1,0:T(8,128)(2,1)S(1)}, u32[]{:S(2)}, u32[]{:S(2)}) collective-permute-start(bf16[300,128]{1,0:T(8,128)(2,1)} %pad_maximum_fusion), channel_id=1, source_target_pairs={{0,2},{1,3},{2,0},{3,1},{4,6},{5,7},{6,4},{7,5},{8,10},{9,11},{10,... | collective-permute-start | bytes 230408 | tf_op jit(solution)/shard_map/ppermute | solution.py:198
  3.1 8.8 %collective-permute-start.17 = (bf16[300,128]{1,0:T(8,128)(2,1)}, bf16[300,128]{1,0:T(8,128)(2,1)S(1)}, u32[]{:S(2)}, u32[]{:S(2)}) collective-permute-start(bf16[300,128]{1,0:T(8,128)(2,1)} %pad_maximum_fusion), channel_id=1, source_target_pairs={{0,1},{1,0},{2,3},{3,2},{4,5},{5,4},{6,7},{7,6},{8,9},{9,8},{10,11... | collective-permute-start | bytes 230408 | tf_op jit(solution)/shard_map/ppermute | solution.py:198
  3.5 12.5 %collective-permute-start.8 = (bf16[8,8,1024]{2,1,0:T(8,128)(2,1)S(1)}, bf16[8,8,1024]{2,1,0:T(8,128)(2,1)S(1)}, u32[]{:S(2)}, u32[]{:S(2)}) collective-permute-start(bf16[8,8,1024]{2,1,0:T(8,128)(2,1)S(1)} %reshape_reshape.3.rest_0_), channel_id=1, source_target_pairs={{0,16},{1,17},{2,18},{3,19},{4,20},{5,21},{6,22},{7,23},{8,24},{9,... | collective-permute-start | bytes 393224 | tf_op jit(solution)/shard_map/ppermute | solution.py:198
  3.9 9.7 %collective-permute-start.12 = (bf16[8,8,1024]{2,1,0:T(8,128)(2,1)S(1)}, bf16[8,8,1024]{2,1,0:T(8,128)(2,1)S(1)}, u32[]{:S(2)}, u32[]{:S(2)}) collective-permute-start(bf16[8,8,1024]{2,1,0:T(8,128)(2,1)S(1)} %reshape_reshape.3.rest_0_), channel_id=1, source_target_pairs={{0,24},{1,25},{2,26},{3,27},{4,28},{5,29},{6,30},{7,31},{8,0},{9,1... | collective-permute-start | bytes 393224 | tf_op jit(solution)/shard_map/ppermute | solution.py:198
  4.3 11.9 %collective-permute-start.4 = (bf16[8,8,1024]{2,1,0:T(8,128)(2,1)S(1)}, bf16[8,8,1024]{2,1,0:T(8,128)(2,1)S(1)}, u32[]{:S(2)}, u32[]{:S(2)}) collective-permute-start(bf16[8,8,1024]{2,1,0:T(8,128)(2,1)S(1)} %reshape_reshape.3.rest_0_), channel_id=1, source_target_pairs={{0,8},{1,9},{2,10},{3,11},{4,12},{5,13},{6,14},{7,15},{8,16},{9,17... | collective-permute-start | bytes 393224 | tf_op jit(solution)/shard_map/ppermute | solution.py:198
  10.2 7.5 %collective-permute-start.2 = (bf16[8,8,1024]{2,1,0:T(8,128)(2,1)S(1)}, bf16[8,8,1024]{2,1,0:T(8,128)(2,1)S(1)}, u32[]{:S(2)}, u32[]{:S(2)}) collective-permute-start(bf16[8,8,1024]{2,1,0:T(8,128)(2,1)S(1)} %reshape_reshape.3.rest_0_), channel_id=1, source_target_pairs={{0,4},{1,5},{2,6},{3,7},{4,0},{5,1},{6,2},{7,3},{8,12},{9,13},{10,... | collective-permute-start | bytes 393224 | tf_op jit(solution)/shard_map/ppermute | solution.py:198
  11.8 1.8 %collective-permute-start.19 = (bf16[300,128]{1,0:T(8,128)(2,1)S(1)}, bf16[300,128]{1,0:T(8,128)(2,1)S(1)}, u32[]{:S(2)}, u32[]{:S(2)}) collective-permute-start(bf16[300,128]{1,0:T(8,128)(2,1)S(1)} %collective-permute-done.18), channel_id=1, source_target_pairs={{0,1},{1,0},{2,3},{3,2},{4,5},{5,4},{6,7},{7,6},{8,9},{9,8},{10,11... | collective-permute-start | bytes 230408 | tf_op jit(solution)/shard_map/ppermute | solution.py:198
  13.6 4.1 %collective-permute-start.1 = (bf16[8,8,1024]{2,1,0:T(8,128)(2,1)S(1)}, bf16[8,8,1024]{2,1,0:T(8,128)(2,1)S(1)}, u32[]{:S(2)}, u32[]{:S(2)}) collective-permute-start(bf16[8,8,1024]{2,1,0:T(8,128)(2,1)S(1)} %reshape_reshape.3.rest_0_), channel_id=1, source_target_pairs={{0,1},{1,0},{2,3},{3,2},{4,5},{5,4},{6,7},{7,6},{8,9},{9,8},{10,11... | collective-permute-start | bytes 393224 | tf_op jit(solution)/shard_map/ppermute | solution.py:198
  13.6 11.5 %collective-permute-start.14 = (bf16[8,8,1024]{2,1,0:T(8,128)(2,1)S(1)}, bf16[8,8,1024]{2,1,0:T(8,128)(2,1)S(1)}, u32[]{:S(2)}, u32[]{:S(2)}) collective-permute-start(bf16[8,8,1024]{2,1,0:T(8,128)(2,1)S(1)} %collective-permute-done.12.rest_12_), channel_id=1, source_target_pairs={{0,4},{1,5},{2,6},{3,7},{4,0},{5,1},{6,2},{7,3},{8,12},{9,13},{10,... | collective-permute-start | bytes 393224 | tf_op jit(solution)/shard_map/ppermute | solution.py:198
  15.9 9.8 %collective-permute-start.13 = (bf16[8,8,1024]{2,1,0:T(8,128)(2,1)S(1)}, bf16[8,8,1024]{2,1,0:T(8,128)(2,1)S(1)}, u32[]{:S(2)}, u32[]{:S(2)}) collective-permute-start(bf16[8,8,1024]{2,1,0:T(8,128)(2,1)S(1)} %collective-permute-done.12.rest_12_), channel_id=1, source_target_pairs={{0,1},{1,0},{2,3},{3,2},{4,5},{5,4},{6,7},{7,6},{8,9},{9,8},{10,11... | collective-permute-start | bytes 393224 | tf_op jit(solution)/shard_map/ppermute | solution.py:198
  16.2 9.4 %collective-permute-start.6 = (bf16[8,8,1024]{2,1,0:T(8,128)(2,1)S(1)}, bf16[8,8,1024]{2,1,0:T(8,128)(2,1)S(1)}, u32[]{:S(2)}, u32[]{:S(2)}) collective-permute-start(bf16[8,8,1024]{2,1,0:T(8,128)(2,1)S(1)} %collective-permute-done.4.rest_4_), channel_id=1, source_target_pairs={{0,4},{1,5},{2,6},{3,7},{4,0},{5,1},{6,2},{7,3},{8,12},{9,13},{10,... | collective-permute-start | bytes 393224 | tf_op jit(solution)/shard_map/ppermute | solution.py:198
  17.7 8.4 %collective-permute-start.5 = (bf16[8,8,1024]{2,1,0:T(8,128)(2,1)S(1)}, bf16[8,8,1024]{2,1,0:T(8,128)(2,1)S(1)}, u32[]{:S(2)}, u32[]{:S(2)}) collective-permute-start(bf16[8,8,1024]{2,1,0:T(8,128)(2,1)S(1)} %collective-permute-done.4.rest_4_), channel_id=1, source_target_pairs={{0,1},{1,0},{2,3},{3,2},{4,5},{5,4},{6,7},{7,6},{8,9},{9,8},{10,11... | collective-permute-start | bytes 393224 | tf_op jit(solution)/shard_map/ppermute | solution.py:198
  17.7 7.4 %collective-permute-start.10 = (bf16[8,8,1024]{2,1,0:T(8,128)(2,1)S(1)}, bf16[8,8,1024]{2,1,0:T(8,128)(2,1)S(1)}, u32[]{:S(2)}, u32[]{:S(2)}) collective-permute-start(bf16[8,8,1024]{2,1,0:T(8,128)(2,1)S(1)} %collective-permute-done.8.rest_8_), channel_id=1, source_target_pairs={{0,4},{1,5},{2,6},{3,7},{4,0},{5,1},{6,2},{7,3},{8,12},{9,13},{10,... | collective-permute-start | bytes 393224 | tf_op jit(solution)/shard_map/ppermute | solution.py:198
  25.1 1.3 %collective-permute-start.9 = (bf16[8,8,1024]{2,1,0:T(8,128)(2,1)S(1)}, bf16[8,8,1024]{2,1,0:T(8,128)(2,1)S(1)}, u32[]{:S(2)}, u32[]{:S(2)}) collective-permute-start(bf16[8,8,1024]{2,1,0:T(8,128)(2,1)S(1)} %collective-permute-done.8.rest_8_), channel_id=1, source_target_pairs={{0,1},{1,0},{2,3},{3,2},{4,5},{5,4},{6,7},{7,6},{8,9},{9,8},{10,11... | collective-permute-start | bytes 393224 | tf_op jit(solution)/shard_map/ppermute | solution.py:198
  25.1 1.9 %collective-permute-start.3 = (bf16[8,8,1024]{2,1,0:T(8,128)(2,1)S(1)}, bf16[8,8,1024]{2,1,0:T(8,128)(2,1)S(1)}, u32[]{:S(2)}, u32[]{:S(2)}) collective-permute-start(bf16[8,8,1024]{2,1,0:T(8,128)(2,1)S(1)} %collective-permute-done.2.rest_2_), channel_id=1, source_target_pairs={{0,1},{1,0},{2,3},{3,2},{4,5},{5,4},{6,7},{7,6},{8,9},{9,8},{10,11... | collective-permute-start | bytes 393224 | tf_op jit(solution)/shard_map/ppermute | solution.py:198
  25.6 1.4 %collective-permute-start.11 = (bf16[8,8,1024]{2,1,0:T(8,128)(2,1)S(1)}, bf16[8,8,1024]{2,1,0:T(8,128)(2,1)S(1)}, u32[]{:S(2)}, u32[]{:S(2)}) collective-permute-start(bf16[8,8,1024]{2,1,0:T(8,128)(2,1)S(1)} %collective-permute-done.10.rest_10_), channel_id=1, source_target_pairs={{0,1},{1,0},{2,3},{3,2},{4,5},{5,4},{6,7},{7,6},{8,9},{9,8},{10,11... | collective-permute-start | bytes 393224 | tf_op jit(solution)/shard_map/ppermute | solution.py:198
  25.7 1.5 %collective-permute-start.15 = (bf16[8,8,1024]{2,1,0:T(8,128)(2,1)S(1)}, bf16[8,8,1024]{2,1,0:T(8,128)(2,1)S(1)}, u32[]{:S(2)}, u32[]{:S(2)}) collective-permute-start(bf16[8,8,1024]{2,1,0:T(8,128)(2,1)S(1)} %collective-permute-done.14.rest_14_), channel_id=1, source_target_pairs={{0,1},{1,0},{2,3},{3,2},{4,5},{5,4},{6,7},{7,6},{8,9},{9,8},{10,11... | collective-permute-start | bytes 393224 | tf_op jit(solution)/shard_map/ppermute | solution.py:198
  26.2 1.3 %collective-permute-start.7 = (bf16[8,8,1024]{2,1,0:T(8,128)(2,1)S(1)}, bf16[8,8,1024]{2,1,0:T(8,128)(2,1)S(1)}, u32[]{:S(2)}, u32[]{:S(2)}) collective-permute-start(bf16[8,8,1024]{2,1,0:T(8,128)(2,1)S(1)} %collective-permute-done.6.rest_6_), channel_id=1, source_target_pairs={{0,1},{1,0},{2,3},{3,2},{4,5},{5,4},{6,7},{7,6},{8,9},{9,8},{10,11... | collective-permute-start | bytes 393224 | tf_op jit(solution)/shard_map/ppermute | solution.py:198
  26.5 8.6 %collective-permute-start = (bf16[64,1024]{1,0:T(8,128)(2,1)S(1)}, bf16[64,1024]{1,0:T(8,128)(2,1)S(1)}, u32[]{:S(2)}, u32[]{:S(2)}) collective-permute-start(bf16[64,1024]{1,0:T(8,128)(2,1)S(1)} %reshape.10.self_own), channel_id=1, source_target_pairs={{0,2},{1,3},{2,0},{3,1},{4,6},{5,7},{6,4},{7,5},{8,10},{9,11},{10,... | collective-permute-start | bytes 393224 | tf_op jit(solution)/shard_map/ppermute | solution.py:198
  27.5 17.3 %copy-start.3 = (s32[1024]{0:T(1024)S(1)}, s32[1024]{0:T(1024)}, u32[]{:S(2)}) copy-start(s32[1024]{0:T(1024)} %param.23) | copy-start | bytes 12292
  27.5 34.4 %copy-start.4 = (s32[1,64]{1,0:T(1,128)S(1)}, s32[1,64]{1,0:T(1,128)}, u32[]{:S(2)}) copy-start(s32[1,64]{1,0:T(1,128)} %param.20) | copy-start | bytes 772
  33.8 5.6 %collective-permute-start.16 = (bf16[64,1024]{1,0:T(8,128)(2,1)S(1)}, bf16[64,1024]{1,0:T(8,128)(2,1)S(1)}, u32[]{:S(2)}, u32[]{:S(2)}) collective-permute-start(bf16[64,1024]{1,0:T(8,128)(2,1)S(1)} %shard_map.118.near_own), channel_id=1, source_target_pairs={{0,2},{1,3},{2,0},{3,1},{4,6},{5,7},{6,4},{7,5},{8,10},{9,11},{10,... | collective-permute-start | bytes 393224 | tf_op jit(solution)/shard_map/ppermute | solution.py:198
  40.2 8.8 %collective-permute-start.23 = (bf16[8,8,1408]{2,1,0:T(8,128)(2,1)S(1)}, bf16[8,8,1408]{2,1,0:T(8,128)(2,1)S(1)}, u32[]{:S(2)}, u32[]{:S(2)}) collective-permute-start(bf16[8,8,1408]{2,1,0:T(8,128)(2,1)S(1)} %bitcast.33), channel_id=1, source_target_pairs={{0,8},{1,9},{2,10},{3,11},{4,12},{5,13},{6,14},{7,15},{8,16},{9,17... | collective-permute-start | bytes 540680 | tf_op jit(solution)/shard_map/ppermute | solution.py:198
  40.3 20.1 %collective-permute-start.27 = (bf16[8,8,1408]{2,1,0:T(8,128)(2,1)S(1)}, bf16[8,8,1408]{2,1,0:T(8,128)(2,1)S(1)}, u32[]{:S(2)}, u32[]{:S(2)}) collective-permute-start(bf16[8,8,1408]{2,1,0:T(8,128)(2,1)S(1)} %bitcast.34), channel_id=1, source_target_pairs={{0,16},{1,17},{2,18},{3,19},{4,20},{5,21},{6,22},{7,23},{8,24},{9,... | collective-permute-start | bytes 540680 | tf_op jit(solution)/shard_map/ppermute | solution.py:198
  44.8 29.4 %collective-permute-start.35 = (bf16[1024,256]{1,0:T(8,128)(2,1)S(1)}, bf16[1024,256]{1,0:T(8,128)(2,1)S(1)}, u32[]{:S(2)}, u32[]{:S(2)}) collective-permute-start(bf16[1024,256]{1,0:T(8,128)(2,1)S(1)} %get-tuple-element.8.rest_0_), channel_id=1, source_target_pairs={{0,1},{1,0},{2,3},{3,2},{4,5},{5,4},{6,7},{7,6},{8,9},{9,8},{10,11... | collective-permute-start | bytes 1572872 | tf_op jit(solution)/shard_map/ppermute | solution.py:198
  45.5 16.4 %collective-permute-start.31 = (bf16[8,8,1408]{2,1,0:T(8,128)(2,1)S(1)}, bf16[8,8,1408]{2,1,0:T(8,128)(2,1)S(1)}, u32[]{:S(2)}, u32[]{:S(2)}) collective-permute-start(bf16[8,8,1408]{2,1,0:T(8,128)(2,1)S(1)} %bitcast.35), channel_id=1, source_target_pairs={{0,24},{1,25},{2,26},{3,27},{4,28},{5,29},{6,30},{7,31},{8,0},{9,1... | collective-permute-start | bytes 540680 | tf_op jit(solution)/shard_map/ppermute | solution.py:198
  47.5 14.5 %collective-permute-start.21 = (bf16[8,8,1408]{2,1,0:T(8,128)(2,1)S(1)}, bf16[8,8,1408]{2,1,0:T(8,128)(2,1)S(1)}, u32[]{:S(2)}, u32[]{:S(2)}) collective-permute-start(bf16[8,8,1408]{2,1,0:T(8,128)(2,1)S(1)} %bitcast.36), channel_id=1, source_target_pairs={{0,4},{1,5},{2,6},{3,7},{4,0},{5,1},{6,2},{7,3},{8,12},{9,13},{10,... | collective-permute-start | bytes 540680 | tf_op jit(solution)/shard_map/ppermute | solution.py:198
  49.0 13.6 %collective-permute-start.20 = (bf16[8,8,1408]{2,1,0:T(8,128)(2,1)S(1)}, bf16[8,8,1408]{2,1,0:T(8,128)(2,1)S(1)}, u32[]{:S(2)}, u32[]{:S(2)}) collective-permute-start(bf16[8,8,1408]{2,1,0:T(8,128)(2,1)S(1)} %bitcast.37), channel_id=1, source_target_pairs={{0,1},{1,0},{2,3},{3,2},{4,5},{5,4},{6,7},{7,6},{8,9},{9,8},{10,11... | collective-permute-start | bytes 540680 | tf_op jit(solution)/shard_map/ppermute | solution.py:198
  60.4 6.3 %collective-permute-start.25 = (bf16[8,8,1408]{2,1,0:T(8,128)(2,1)S(1)}, bf16[8,8,1408]{2,1,0:T(8,128)(2,1)S(1)}, u32[]{:S(2)}, u32[]{:S(2)}) collective-permute-start(bf16[8,8,1408]{2,1,0:T(8,128)(2,1)S(1)} %collective-permute-done.23.rest_4_), channel_id=1, source_target_pairs={{0,4},{1,5},{2,6},{3,7},{4,0},{5,1},{6,2},{7,3},{8,12},{9,13},{10,... | collective-permute-start | bytes 540680 | tf_op jit(solution)/shard_map/ppermute | solution.py:198
  61.9 12.2 %collective-permute-start.24 = (bf16[8,8,1408]{2,1,0:T(8,128)(2,1)S(1)}, bf16[8,8,1408]{2,1,0:T(8,128)(2,1)S(1)}, u32[]{:S(2)}, u32[]{:S(2)}) collective-permute-start(bf16[8,8,1408]{2,1,0:T(8,128)(2,1)S(1)} %collective-permute-done.23.rest_4_), channel_id=1, source_target_pairs={{0,1},{1,0},{2,3},{3,2},{4,5},{5,4},{6,7},{7,6},{8,9},{9,8},{10,11... | collective-permute-start | bytes 540680 | tf_op jit(solution)/shard_map/ppermute | solution.py:198
  62.0 8.6 %collective-permute-start.29 = (bf16[8,8,1408]{2,1,0:T(8,128)(2,1)S(1)}, bf16[8,8,1408]{2,1,0:T(8,128)(2,1)S(1)}, u32[]{:S(2)}, u32[]{:S(2)}) collective-permute-start(bf16[8,8,1408]{2,1,0:T(8,128)(2,1)S(1)} %collective-permute-done.27.rest_8_), channel_id=1, source_target_pairs={{0,4},{1,5},{2,6},{3,7},{4,0},{5,1},{6,2},{7,3},{8,12},{9,13},{10,... | collective-permute-start | bytes 540680 | tf_op jit(solution)/shard_map/ppermute | solution.py:198
  62.6 11.0 %collective-permute-start.33 = (bf16[8,8,1408]{2,1,0:T(8,128)(2,1)S(1)}, bf16[8,8,1408]{2,1,0:T(8,128)(2,1)S(1)}, u32[]{:S(2)}, u32[]{:S(2)}) collective-permute-start(bf16[8,8,1408]{2,1,0:T(8,128)(2,1)S(1)} %collective-permute-done.31.rest_12_), channel_id=1, source_target_pairs={{0,4},{1,5},{2,6},{3,7},{4,0},{5,1},{6,2},{7,3},{8,12},{9,13},{10,... | collective-permute-start | bytes 540680 | tf_op jit(solution)/shard_map/ppermute | solution.py:198
  66.7 6.9 %collective-permute-start.22 = (bf16[8,8,1408]{2,1,0:T(8,128)(2,1)S(1)}, bf16[8,8,1408]{2,1,0:T(8,128)(2,1)S(1)}, u32[]{:S(2)}, u32[]{:S(2)}) collective-permute-start(bf16[8,8,1408]{2,1,0:T(8,128)(2,1)S(1)} %collective-permute-done.21.rest_2_), channel_id=1, source_target_pairs={{0,1},{1,0},{2,3},{3,2},{4,5},{5,4},{6,7},{7,6},{8,9},{9,8},{10,11... | collective-permute-start | bytes 540680 | tf_op jit(solution)/shard_map/ppermute | solution.py:198
  70.6 6.2 %collective-permute-start.28 = (bf16[8,8,1408]{2,1,0:T(8,128)(2,1)S(1)}, bf16[8,8,1408]{2,1,0:T(8,128)(2,1)S(1)}, u32[]{:S(2)}, u32[]{:S(2)}) collective-permute-start(bf16[8,8,1408]{2,1,0:T(8,128)(2,1)S(1)} %collective-permute-done.27.rest_8_), channel_id=1, source_target_pairs={{0,1},{1,0},{2,3},{3,2},{4,5},{5,4},{6,7},{7,6},{8,9},{9,8},{10,11... | collective-permute-start | bytes 540680 | tf_op jit(solution)/shard_map/ppermute | solution.py:198
  73.6 3.2 %collective-permute-start.32 = (bf16[8,8,1408]{2,1,0:T(8,128)(2,1)S(1)}, bf16[8,8,1408]{2,1,0:T(8,128)(2,1)S(1)}, u32[]{:S(2)}, u32[]{:S(2)}) collective-permute-start(bf16[8,8,1408]{2,1,0:T(8,128)(2,1)S(1)} %collective-permute-done.31.rest_12_), channel_id=1, source_target_pairs={{0,1},{1,0},{2,3},{3,2},{4,5},{5,4},{6,7},{7,6},{8,9},{9,8},{10,11... | collective-permute-start | bytes 540680 | tf_op jit(solution)/shard_map/ppermute | solution.py:198
  73.6 3.2 %collective-permute-start.26 = (bf16[8,8,1408]{2,1,0:T(8,128)(2,1)S(1)}, bf16[8,8,1408]{2,1,0:T(8,128)(2,1)S(1)}, u32[]{:S(2)}, u32[]{:S(2)}) collective-permute-start(bf16[8,8,1408]{2,1,0:T(8,128)(2,1)S(1)} %collective-permute-done.25.rest_6_), channel_id=1, source_target_pairs={{0,1},{1,0},{2,3},{3,2},{4,5},{5,4},{6,7},{7,6},{8,9},{9,8},{10,11... | collective-permute-start | bytes 540680 | tf_op jit(solution)/shard_map/ppermute | solution.py:198
  74.1 2.7 %collective-permute-start.30 = (bf16[8,8,1408]{2,1,0:T(8,128)(2,1)S(1)}, bf16[8,8,1408]{2,1,0:T(8,128)(2,1)S(1)}, u32[]{:S(2)}, u32[]{:S(2)}) collective-permute-start(bf16[8,8,1408]{2,1,0:T(8,128)(2,1)S(1)} %collective-permute-done.29.rest_10_), channel_id=1, source_target_pairs={{0,1},{1,0},{2,3},{3,2},{4,5},{5,4},{6,7},{7,6},{8,9},{9,8},{10,11... | collective-permute-start | bytes 540680 | tf_op jit(solution)/shard_map/ppermute | solution.py:198
  74.2 2.7 %collective-permute-start.34 = (bf16[8,8,1408]{2,1,0:T(8,128)(2,1)S(1)}, bf16[8,8,1408]{2,1,0:T(8,128)(2,1)S(1)}, u32[]{:S(2)}, u32[]{:S(2)}) collective-permute-start(bf16[8,8,1408]{2,1,0:T(8,128)(2,1)S(1)} %collective-permute-done.33.rest_14_), channel_id=1, source_target_pairs={{0,1},{1,0},{2,3},{3,2},{4,5},{5,4},{6,7},{7,6},{8,9},{9,8},{10,11... | collective-permute-start | bytes 540680 | tf_op jit(solution)/shard_map/ppermute | solution.py:198
  74.6 2.3 %copy-start.2 = (s32[1024,512]{1,0:T(8,128)S(1)}, s32[1024,512]{1,0:T(8,128)}, u32[]{:S(2)}) copy-start(s32[1024,512]{1,0:T(8,128)} %adj_ref.3) | copy-start | bytes 6291460
  83.4 6.6 %collective-permute-start.36 = (bf16[86,1024]{1,0:T(8,128)(2,1)S(1)}, bf16[86,1024]{1,0:T(8,128)(2,1)S(1)}, u32[]{:S(2)}, u32[]{:S(2)}) collective-permute-start(bf16[86,1024]{1,0:T(8,128)(2,1)S(1)} %shard_map.119), channel_id=1, source_target_pairs={{0,2},{1,3},{2,0},{3,1},{4,6},{5,7},{6,4},{7,5},{8,10},{9,11},{10,... | collective-permute-start | bytes 528392 | tf_op jit(solution)/shard_map/ppermute | solution.py:198
where the time goes:
time: 91.3 us; the launch traced here: 90.9 us
  waiting for transfers between devices  38.9 us (43%)
  starting transfers between devices  27.4 us (30%)
  Pallas kernels  15.7 us (17%)
  other arithmetic  5.84 us (6%)
  between operations  1.59 us (2%)
  local copies, waits for them, and re-layouts  1.48 us (2%)
    ppermute x37, waiting for transfers between devices, move(): return lax.ppermute(array, MESH_AXES, shift_perm(grid, which, by))  38.9 us
    ppermute x37, starting transfers between devices, move(): return lax.ppermute(array, MESH_AXES, shift_perm(grid, which, by))  27.4 us
    pallas_call x2, Pallas kernels, mean_call(): pl.pallas_call(functools.partial(kernel, width, len(pieces)), in_specs=[S...  12.7 us
    pallas_call x1, Pallas kernels, per_device(): own_call(place.reshape(1, seeds), weight_own, *[here(h) for h in hidden_p...  2.19 us
  transfers between devices with their start and end apart: 37, of which 13 were waited for; matrix products, arithmetic and copies ran while one was open for 5% of the time, Pallas kernels for 9%

commit v1 on v0

v1 whole, which is shorter than its diff:
```python
import functools

import jax
import jax.numpy as jnp
from jax import lax
from jax.experimental import pallas as pl
from jax.experimental.pallas import tpu as pltpu
from jax.sharding import PartitionSpec as P


BLK = 128
BITS = 16
PLANES = 15
WORDS = BLK // BITS
LANES = 128
MESH_AXES = ("dom", "col", "batch")
VMEM = pl.BlockSpec(memory_space=pltpu.VMEM)
SMEM = pl.BlockSpec(memory_space=pltpu.SMEM)
ANY = pl.BlockSpec(memory_space=pl.ANY)
PARAMS = pltpu.CompilerParams(vmem_limit_bytes=20 * 2**20)


def lanes_for(width):
    need = max((PLANES - 1) * width + LANES, BITS * width if width % 64 == 0 else 0)
    return -(-need // LANES) * LANES


def paired(size):
    return size & (size - 1) == 0


def shift_perm(sizes, which, by):
    pairs = []
    total = 1
    for size in sizes:
        total *= size
    for source in range(total):
        place = []
        rest = source
        for size in reversed(sizes):
            place.append(rest % size)
            rest //= size
        place = place[::-1]
        size = sizes[which]
        place[which] = place[which] ^ by if paired(size) else (place[which] + by) % size
        target = 0
        for size, at in zip(sizes, place):
            target = target * size + at
        pairs.append((source, target))
    return pairs


def pack_planes(tall_ref, out_ref, width, planes):
    words = out_ref.shape[0]
    for i in range(planes):
        piece = tall_ref[pl.ds(i, words, stride=BITS), :]
        out_ref[:, i * width : (i + 1) * width] = piece[:, :width]


def fetch_words(adj_ref, words_ref, sem):
    rows = adj_ref.shape[0] // sem.shape[0]
    copies = [
        pltpu.make_async_copy(adj_ref.at[pl.ds(n * rows, rows)], words_ref.at[pl.ds(n * rows, rows)], sem.at[n])
        for n in range(sem.shape[0])
    ]
    for copy in copies:
        copy.start()
    return copies


def behind(at, by, size):
    return lax.bitwise_xor(at, jnp.int32(by)) if paired(size) else lax.rem(at + size - by, size)


def owner_of(grid, piece, place_ref):
    outer, inner, _, n_batch = grid
    ko, ki, kb = piece // (inner * n_batch), piece // n_batch % inner, piece % n_batch
    dom_at, batch_at = place_ref[0], place_ref[2]
    outer_at = behind(lax.div(dom_at, inner), ko, outer)
    inner_at = behind(lax.rem(dom_at, inner), ki, inner)
    return (outer_at * inner + inner_at) * n_batch + behind(batch_at, kb, n_batch)


def invert(need_ref, inverse_ref):
    listed = need_ref.shape[0]

    def clear(g, _):
        inverse_ref[g] = listed
        return 0

    def enter(b, _):
        inverse_ref[need_ref[b]] = b
        return 0

    lax.fori_loop(0, inverse_ref.shape[0], clear, 0, unroll=8)
    lax.fori_loop(0, listed, enter, 0, unroll=8)


def pick_blocks(grid, place_ref, inverse_ref, pieces, picked_ref, cleared=()):
    for n, piece in pieces:
        blocks = piece.shape[0]
        owner = owner_of(grid, n, place_ref)
        for k in range(blocks):
            at = pl.multiple_of(inverse_ref[owner * blocks + k] * WORDS, WORDS)
            picked_ref[pl.ds(at, WORDS), :] = piece[k].astype(jnp.float32)
    for n in cleared:
        owner = owner_of(grid, n, place_ref)
        for k in range(blocks):
            at = pl.multiple_of(inverse_ref[owner * blocks + k] * WORDS, WORDS)
            picked_ref[pl.ds(at, WORDS), :] = jnp.zeros((WORDS, picked_ref.shape[1]), jnp.float32)


def below(need_ref, bound):
    def add(b, total):
        return total + jnp.where(need_ref[b] < bound, 1, 0)

    return lax.fori_loop(0, need_ref.shape[0], add, 0, unroll=8)


def turns_of(outer):
    return list(range(1, outer))


def late_parts(grid):
    outer, inner, _, n_batch = grid
    return [
        [(ko * inner + inner - 1) * n_batch + kb for kb in range(n_batch)] for ko in ([0] + turns_of(outer))[-1:]
    ]


def late_spans(grid, blocks, place_ref, need_ref):
    n_batch = grid[3]
    spans = []
    for part in late_parts(grid):
        first = lax.div(owner_of(grid, part[0], place_ref), n_batch) * (n_batch * blocks)
        spans.append((below(need_ref, first), below(need_ref, first + n_batch * blocks)))
    return spans


def multiply_planes(short_ref, picked_ref, total_ref, width):
    short = short_ref.shape
    one, zero = jnp.ones(short, jnp.bfloat16), jnp.zeros(short, jnp.bfloat16)
    joined = max(1, 256 // short[1])
    for i in range(0, PLANES, joined):
        masks, tables = [], []
        for k in range(i, min(i + joined, PLANES)):
            tables.append(picked_ref[: short[1], k * width : k * width + LANES].astype(jnp.bfloat16))
            masks.append(jnp.where(short_ref[...] == jnp.int16(1 << k), one, zero))
        mask, table = jnp.concatenate(masks, axis=1), jnp.concatenate(tables, axis=0)
        part = jnp.dot(mask, table, preferred_element_type=jnp.float32)
        if i == 0:
            total_ref[...] = part
        else:
            total_ref[...] += part


def mean_kernel(grid, width, n_pieces, place_ref, need_ref, count_ref, adj_ref, *rest):
    pieces, out_ref = rest[:n_pieces], rest[n_pieces]
    words_ref, short_ref, picked_ref, total_ref, wide_ref, inverse_ref, sem = rest[n_pieces + 1 :]
    copies = fetch_words(adj_ref, words_ref, sem)
    invert(need_ref, inverse_ref)
    pick_blocks(grid, place_ref, inverse_ref, list(enumerate(pieces)), picked_ref)
    rows = words_ref.shape[0] // len(copies)
    degrees = []
    for n, copy in enumerate(copies):
        copy.wait()
        words = words_ref[n * rows : (n + 1) * rows, :]
        column = lax.broadcasted_iota(jnp.int32, words.shape, 1)
        words = jnp.where(column < count_ref[0] * WORDS, words, 0)
        degrees.append(jnp.sum(jnp.where(words != 0, 1.0, 0.0), axis=1, keepdims=True))
        short_ref[n * rows : (n + 1) * rows, :] = words.astype(jnp.int16)
    multiply_planes(short_ref, picked_ref, total_ref, width)
    total_ref[...] = total_ref[...] / jnp.maximum(jnp.concatenate(degrees, axis=0), 1.0)
    pack_planes(total_ref, wide_ref, width, BITS)
    out_ref[...] = wide_ref[...].astype(jnp.bfloat16)


def prepare_kernel(grid, blocks, place_ref, need_ref, count_ref, adj_ref, short_ref, late_ref, degree_ref, words_ref, sem):
    copies = fetch_words(adj_ref, words_ref, sem)
    spans = late_spans(grid, blocks, place_ref, need_ref)
    rows = words_ref.shape[0] // len(copies)
    whole = words_ref.shape[1]
    window = late_ref.shape[1] // len(spans)
    for n, copy in enumerate(copies):
        copy.wait()
        at = slice(n * rows, (n + 1) * rows)
        words = words_ref[at, :]
        column = lax.broadcasted_iota(jnp.int32, words.shape, 1)
        words = jnp.where(column < count_ref[0] * WORDS, words, 0)
        degree = jnp.sum(jnp.where(words != 0, 1.0, 0.0), axis=1, keepdims=True)
        degree_ref[at, :] = jnp.broadcast_to(jnp.maximum(degree, 1.0), (rows, LANES))
        early = words
        for k, (low, high) in enumerate(spans):
            early = jnp.where((column >= low * WORDS) & (column < high * WORDS), 0, early)
            turned = pltpu.roll(words, lax.rem(whole - low * WORDS, whole), 1)[:, :window]
            inside = lax.broadcasted_iota(jnp.int32, turned.shape, 1) < (high - low) * WORDS
            late_ref[at, k * window : (k + 1) * window] = jnp.where(inside, turned, 0)
        short_ref[at, :] = early.astype(jnp.int16)


def main_kernel(grid, width, n_pieces, place_ref, need_ref, short_ref, *rest):
    late = [n for part in late_parts(grid) for n in part]
    early = [n for n in range(n_pieces) if n not in late]
    pieces, total_ref = rest[: len(early)], rest[len(early)]
    picked_ref, inverse_ref = rest[len(early) + 1 :]
    invert(need_ref, inverse_ref)
    pick_blocks(grid, place_ref, inverse_ref, list(zip(early, pieces)), picked_ref, late)
    multiply_planes(short_ref, picked_ref, total_ref, width)


def late_kernel(grid, width, place_ref, need_ref, words_ref, degree_ref, main_ref, own_ref, *rest):
    parts = late_parts(grid)
    n_late = sum(len(part) for part in parts)
    pieces, out_ref = rest[:n_late], rest[n_late]
    picked_ref, short_ref, total_ref, inverse_ref = rest[n_late + 1 :]
    blocks = pieces[0].shape[0]
    picked_ref[...] = jnp.zeros_like(picked_ref)
    invert(need_ref, inverse_ref)
    spans = late_spans(grid, blocks, place_ref, need_ref)
    listed = need_ref.shape[0]
    window = words_ref.shape[1] // len(parts) // WORDS
    spare = len(parts) * window
    used = 0
    for k, part in enumerate(parts):
        for n in part:
            owner = owner_of(grid, n, place_ref)
            for g in range(blocks):
                at = inverse_ref[owner * blocks + g]
                at = jnp.where(at == listed, spare, at - spans[k][0] + k * window)
                picked_ref[pl.ds(pl.multiple_of(at * WORDS, WORDS), WORDS), :] = pieces[used][g].astype(jnp.float32)
            used += 1
    short_ref[...] = words_ref[...].astype(jnp.int16)
    multiply_planes(short_ref, picked_ref, total_ref, width)
    mean = (main_ref[...] + total_ref[...]) / degree_ref[...]
    out_ref[...] = (mean.T + own_ref[...])[:width, :].astype(jnp.bfloat16)


def here(array):
    return pltpu.with_memory_space_constraint(array, pltpu.VMEM)


def cost(flops, count):
    return pl.CostEstimate(flops=flops, bytes_accessed=count, transcendentals=0)


def stay(array):
    return pltpu.with_memory_space_constraint(array, pltpu.HBM)


def mean_call(grid, place, need, count, adjacency, pieces, width):
    rows, row_words = adjacency.shape
    blocks, _, lanes = pieces[0].shape
    return pl.pallas_call(
        functools.partial(mean_kernel, grid, width, len(pieces)),
        in_specs=[SMEM] * 3 + [ANY] + [VMEM] * len(pieces),
        out_specs=VMEM,
        out_shape=pltpu.VMEM((rows // BITS, lanes), jnp.bfloat16),
        scratch_shapes=[
            pltpu.VMEM((rows, row_words), jnp.int32),
            pltpu.VMEM((rows, row_words), jnp.int16),
            pltpu.VMEM((row_words + WORDS, lanes), jnp.float32),
            pltpu.VMEM((rows, LANES), jnp.float32),
            pltpu.VMEM((rows // BITS, lanes), jnp.float32),
            pltpu.SMEM((len(pieces) * blocks,), jnp.int32),
            pltpu.SemaphoreType.DMA((4,)),
        ],
        compiler_params=PARAMS,
        cost_estimate=cost(2 * rows * row_words * PLANES * LANES, 4 * rows * row_words),
        name="mean_first",
    )(place, need, count, stay(adjacency), *[here(p) for p in pieces])


def prepare_call(grid, place, need, count, adjacency, blocks):
    rows, row_words = adjacency.shape
    window = min(grid[3] * blocks * WORDS, row_words) * len(late_parts(grid))
    return pl.pallas_call(
        functools.partial(prepare_kernel, grid, blocks),
        in_specs=[SMEM] * 3 + [ANY],
        out_specs=[VMEM] * 3,
        out_shape=[
            pltpu.VMEM((rows, row_words), jnp.int16),
            pltpu.VMEM((rows, window), jnp.int32),
            pltpu.VMEM((rows, LANES), jnp.float32),
        ],
        scratch_shapes=[pltpu.VMEM((rows, row_words), jnp.int32), pltpu.SemaphoreType.DMA((4,))],
        compiler_params=PARAMS,
        cost_estimate=cost(2 * rows * row_words * LANES, 4 * rows * row_words),
        name="prepare",
    )(place, need, count, stay(adjacency))


def split_mean_calls(grid, place, need, prepared, pieces, own, width):
    short, late_words, degree = prepared
    rows, row_words = short.shape
    blocks, _, lanes = pieces[0].shape
    late = [n for part in late_parts(grid) for n in part]
    early = [n for n in range(len(pieces)) if n not in late]
    inverse = pltpu.SMEM((len(pieces) * blocks,), jnp.int32)
    total = pl.pallas_call(
        functools.partial(main_kernel, grid, width, len(pieces)),
        in_specs=[SMEM] * 2 + [VMEM] * (1 + len(early)),
        out_specs=VMEM,
        out_shape=pltpu.VMEM((rows, LANES), jnp.float32),
        scratch_shapes=[pltpu.VMEM((row_words + WORDS, lanes), jnp.float32), inverse],
        compiler_params=PARAMS,
        cost_estimate=cost(2 * rows * row_words * PLANES * LANES, 4 * rows * row_words),
        name="mean_main",
    )(place, need, here(short), *[here(pieces[n]) for n in early])
    late_cols = late_words.shape[1]
    return pl.pallas_call(
        functools.partial(late_kernel, grid, width),
        in_specs=[SMEM] * 2 + [VMEM] * (4 + len(late)),
        out_specs=VMEM,
        out_shape=pltpu.VMEM((width, rows), jnp.bfloat16),
        scratch_shapes=[
            pltpu.VMEM((late_cols + WORDS, lanes), jnp.float32),
            pltpu.VMEM((rows, late_cols), jnp.int16),
            pltpu.VMEM((rows, LANES), jnp.float32),
            inverse,
        ],
        compiler_params=PARAMS,
        cost_estimate=cost(2 * rows * late_cols * PLANES * LANES, 4 * rows * LANES),
        name="mean_late",
    )(place, need, here(late_words), here(degree), here(total), here(own), *[here(pieces[n]) for n in late])


def picked_by(values, at):
    chosen = values[0]
    for n in range(1, len(values)):
        chosen = jnp.where(at == n, values[n], chosen)
    return chosen


def hidden_kernel(width, classes, spare, grid, place_ref, *rest):
    _, _, n_col, n_batch = grid
    n_parts = 2 * n_col
    parts, packs = rest[:n_parts], rest[n_parts : n_parts + n_col * n_batch]
    hidden_ref, wide_ref, own_weight_ref, rows_ref, tall_ref, scratch_ref = rest[n_parts + n_col * n_batch :]
    col_at, batch_at = place_ref[1], place_ref[2]
    words = parts[0].shape[0]

    def weights(back, owner, low, count):
        found = [packs[back * n_batch + k][low : low + count, :] for k in range(n_batch)]
        return picked_by(found, lax.rem(batch_at + n_batch - owner, n_batch))

    first = [
        jnp.concatenate([weights(back, owner, half * width, width) for owner in range(n_batch)], axis=1)
        for half in range(2)
        for back in range(n_col)
    ]

    def class_weights(low):
        by_back = [weights(back, col_at, low, spare) for back in range(n_col)]
        return jnp.concatenate(
            [picked_by(by_back, lax.rem(col_at + n_col - owner, n_col)) for owner in range(n_col)], axis=1
        )

    own_weight_ref[...] = class_weights(2 * width)
    far_weight = class_weights(2 * width + spare)
    for i in range(BITS):
        for n, part in enumerate(parts):
            rows_ref[pl.ds(i * words, words), n * width : (n + 1) * width] = part[:, i * width : (i + 1) * width]
    hidden = jnp.dot(rows_ref[...], jnp.concatenate(first, axis=0), preferred_element_type=jnp.float32)
    hidden = jnp.maximum(hidden, 0.0).astype(jnp.bfloat16)
    hidden_ref[...] = hidden
    tall_ref[...] = lax.dot_general(
        hidden, far_weight, (((1,), (1,)), ((), ())), preferred_element_type=jnp.float32
    )
    scratch_ref[...] = jnp.zeros_like(scratch_ref)
    for i in range(PLANES):
        scratch_ref[:, i * classes : (i + 1) * classes] = tall_ref[pl.ds(i * words, words), :classes]
    wide_ref[...] = scratch_ref[...].astype(jnp.bfloat16)


def own_kernel(seed_ref, weight_ref, *rest):
    hidden_refs, out_ref = rest[:-1], rest[-1]
    total = jnp.zeros((weight_ref.shape[0], out_ref.shape[1]), jnp.float32)
    for n, hidden_ref in enumerate(hidden_refs):
        rows = hidden_ref.shape[0]
        every = lax.dot_general(
            weight_ref[...], hidden_ref[...], (((1,), (1,)), ((), ())), preferred_element_type=jnp.float32
        )
        high = every.astype(jnp.bfloat16)
        low = (every - high.astype(jnp.float32)).astype(jnp.bfloat16)
        place = lax.broadcasted_iota(jnp.int32, (rows, seed_ref.shape[1]), 0) + n * rows
        chosen = jnp.where(place == seed_ref[...], 1.0, 0.0).astype(jnp.bfloat16)
        total += jnp.dot(high, chosen, preferred_element_type=jnp.float32)
        total += jnp.dot(low, chosen, preferred_element_type=jnp.float32)
    out_ref[...] = jnp.zeros_like(out_ref)
    out_ref[: total.shape[0], :] = total


def per_device(
    grid,
    features,
    self_weight1,
    neigh_weight1,
    need_first,
    count_first,
    adjacency_first,
    self_weight2,
    neigh_weight2,
    need_second,
    count_second,
    adjacency_second,
    seed_rows,
):
    _, _, n_col, n_batch = grid
    dom_at, col_at, batch_at = (lax.axis_index(a) for a in MESH_AXES)

    def move(array, which, by):
        return lax.ppermute(array, MESH_AXES, shift_perm(grid, which, by))

    def ring(array, which):
        return [array] + [move(array, which, by) for by in range(1, grid[which])]

    def gather_blocks(piece):
        return [last for first in ring(piece, 0) for second in ring(first, 1) for last in ring(second, 3)]

    def in_order(relative, at):
        n = len(relative)
        ordered = []
        for owner in range(n):
            chosen = relative[0]
            for back in range(1, n):
                chosen = jnp.where((at - owner) % n == back, relative[back], chosen)
            ordered.append(chosen)
        return ordered

    width = features.shape[1]
    rows = adjacency_first.shape[0]
    words = rows // BITS
    lanes = lanes_for(width)
    blocks = rows // BLK

    place = jnp.stack([dom_at, col_at, batch_at])
    prepared = prepare_call(grid, place, need_second[0], count_second, adjacency_second, blocks)

    own = lax.dynamic_slice_in_dim(features, batch_at * rows, rows, 0).reshape(words, BITS * width)
    if lanes > BITS * width:
        own = jnp.pad(own, ((0, 0), (0, lanes - BITS * width)))
    pieces_first = gather_blocks(own.reshape(blocks, WORDS, lanes))

    self_parts = ring(own, 2)
    class_cols = self_weight2.shape[1]
    classes = class_cols * n_batch // n_col
    spare = -(-class_cols // 16) * 16
    tall2 = [jnp.pad(w.T, ((0, spare - class_cols), (0, 0))) for w in (self_weight2, neigh_weight2)]
    packed = jnp.concatenate([self_weight1, neigh_weight1, *tall2], axis=0)
    packs = [p for a in ring(packed, 2) for p in ring(a, 3)]

    near = mean_call(grid, place, need_first[0], count_first, adjacency_first, pieces_first, width)
    near_parts = ring(near, 2)
    wide = lanes_for(classes)
    hidden_cols = self_weight1.shape[1] * n_batch
    hidden, scores, weight_own = pl.pallas_call(
        functools.partial(hidden_kernel, width, classes, spare, grid),
        in_specs=[SMEM] + [VMEM] * (2 * n_col + n_col * n_batch),
        out_specs=[VMEM] * 3,
        out_shape=[
            pltpu.VMEM((rows, hidden_cols), jnp.bfloat16),
            pltpu.VMEM((words, wide), jnp.bfloat16),
            pltpu.VMEM((spare, hidden_cols), jnp.bfloat16),
        ],
        scratch_shapes=[
            pltpu.VMEM((rows, 2 * n_col * width), jnp.bfloat16),
            pltpu.VMEM((rows, spare), jnp.float32),
            pltpu.VMEM((words, wide), jnp.float32),
        ],
        compiler_params=PARAMS,
        name="hidden",
    )(place, *[here(a) for a in (*self_parts, *near_parts, *packs)])

    pieces_second = gather_blocks(scores.reshape(blocks, WORDS, wide))
    inside = seed_rows % rows
    seed_at = ((batch_at - seed_rows // rows) % n_batch) * rows + (inside % BITS) * words + inside // BITS
    seeds = seed_rows.shape[0]
    own_call = pl.pallas_call(
        own_kernel,
        in_specs=[VMEM] * (2 + n_batch),
        out_specs=VMEM,
        out_shape=pltpu.VMEM((LANES, seeds), jnp.float32),
        compiler_params=PARAMS,
        cost_estimate=pl.CostEstimate(
            flops=12 * rows * n_batch * seeds * LANES, bytes_accessed=4 * classes * seeds, transcendentals=0
        ),
        name="own_rows",
    )
    hidden_parts = ring(hidden, 3)
    own_second = own_call(seed_at.reshape(1, seeds), here(weight_own), *[here(h) for h in hidden_parts])
    half = split_mean_calls(grid, place, need_second[0], prepared, pieces_second, own_second, classes)
    logits = jnp.concatenate(in_order(ring(half, 2), col_at), axis=0)
    return logits.astype(jnp.float32).T


def solution(mesh):
    sizes = tuple(mesh.shape[a] for a in MESH_AXES)
    inner = 2 if sizes[0] % 2 == 0 else 1
    grid = (sizes[0] // inner, inner, sizes[1], sizes[2])
    placed = (
        P("dom", "col"),
        P("col", "batch"),
        P("col", "batch"),
        P(("dom", "batch"), None),
        P(("dom", "batch")),
        P(("dom", "batch"), None),
        P("col", "batch"),
        P("col", "batch"),
        P(("dom", "batch"), None),
        P(("dom", "batch")),
        P(("dom", "batch"), None),
        P(("dom", "batch")),
    )

    def body(*args):
        return per_device(grid, *args)

    return jax.shard_map(
        body, mesh=mesh, in_specs=placed, out_specs=P(("dom", "batch"), None), check_vma=False
    )
```

time: 91.3 us -> 94.9 us (1.039)
  the two profiles are of different devices: /device:TPU:24 before, /device:TPU:0 now
where the time goes in v1:
time: 94.9 us; the launch traced here: 94.6 us
  waiting for transfers between devices  39.6 us (42%)
  starting transfers between devices  28.4 us (30%)
  Pallas kernels  21.2 us (22%)
  local copies, waits for them, and re-layouts  2.19 us (2%)
  other arithmetic  1.84 us (2%)
  between operations  1.46 us (2%)
    ppermute x37, waiting for transfers between devices, move(): return lax.ppermute(array, MESH_AXES, shift_perm(grid, which, by))  39.6 us
    ppermute x37, starting transfers between devices, move(): return lax.ppermute(array, MESH_AXES, shift_perm(grid, which, by))  28.4 us
    pallas_call x1, Pallas kernels, mean_call(): pl.pallas_call(functools.partial(mean_kernel, grid, width, len(pieces)),...  6.52 us
    pallas_call x1, Pallas kernels, split_mean_calls(): pl.pallas_call(functools.partial(main_kernel, grid, width, len(pieces)),...  5.77 us
    pallas_call x1, Pallas kernels, prepare_call(): pl.pallas_call(functools.partial(prepare_kernel, grid, blocks), in_specs=...  2.86 us
    pallas_call x1, Pallas kernels, split_mean_calls(): pl.pallas_call(functools.partial(late_kernel, grid, width), in_specs=[SME...  2.44 us
    pallas_call x1, Pallas kernels, per_device(): own_call(seed_at.reshape(1, seeds), here(weight_own), *[here(h) for h in...  2.21 us
  transfers between devices with their start and end apart: 37, of which 12 were waited for; matrix products, arithmetic and copies ran while one was open for 1% of the time, Pallas kernels for 18%

profile of v1, /device:TPU:0, one launch (start us, length us, event | category | flops | bytes accessed | tf_op | source)
XLA Modules:
  0.0 94.6 jit_solution(14430946512989199871)
XLA Ops:
  0.0 0.9 %copy-done = bf16[2048,64]{0,1:T(8,128)(2,1)S(1)} copy-done((bf16[2048,64]{0,1:T(8,128)(2,1)S(1)}, bf16[2048,64]{0,1:T(8,128)(2,1)}, u32[]{:S(2)}) %copy-start) | copy-done | bytes 262168
  1.0 0.2 copy.15
  1.1 0.2 reshape_reshape.3.rest_0_
  1.4 4.1 %collective-permute-start.8 = (bf16[8,8,1024]{2,1,0:T(8,128)(2,1)S(1)}, bf16[8,8,1024]{2,1,0:T(8,128)(2,1)S(1)}, u32[]{:S(2)}, u32[]{:S(2)}) collective-permute-start(bf16[8,8,1024]{2,1,0:T(8,128)(2,1)S(1)} %reshape_reshape.3.rest_0_), channel_id=1, source_target_pairs={{0,16},{1,17},{2,18},{3,19},{4,20},{5,21},{6,22},{7,23},{8,24},{9,... | collective-permute-start | bytes 393224 | tf_op jit(solution)/shard_map/ppermute | solution.py:412
  5.5 1.3 %collective-permute-start.12 = (bf16[8,8,1024]{2,1,0:T(8,128)(2,1)S(1)}, bf16[8,8,1024]{2,1,0:T(8,128)(2,1)S(1)}, u32[]{:S(2)}, u32[]{:S(2)}) collective-permute-start(bf16[8,8,1024]{2,1,0:T(8,128)(2,1)S(1)} %reshape_reshape.3.rest_0_), channel_id=1, source_target_pairs={{0,24},{1,25},{2,26},{3,27},{4,28},{5,29},{6,30},{7,31},{8,16},{9,... | collective-permute-start | bytes 393224 | tf_op jit(solution)/shard_map/ppermute | solution.py:412
  6.8 0.2 collective-permute-start.4
  7.1 1.5 %collective-permute-start.2 = (bf16[8,8,1024]{2,1,0:T(8,128)(2,1)S(1)}, bf16[8,8,1024]{2,1,0:T(8,128)(2,1)S(1)}, u32[]{:S(2)}, u32[]{:S(2)}) collective-permute-start(bf16[8,8,1024]{2,1,0:T(8,128)(2,1)S(1)} %reshape_reshape.3.rest_0_), channel_id=1, source_target_pairs={{0,4},{1,5},{2,6},{3,7},{4,0},{5,1},{6,2},{7,3},{8,12},{9,13},{10,... | collective-permute-start | bytes 393224 | tf_op jit(solution)/shard_map/ppermute | solution.py:412
  8.6 0.0 collective-permute-start.1
  8.6 6.9 %collective-permute-done.8.rest_8_ = bf16[8,8,1024]{2,1,0:T(8,128)(2,1)S(1)} collective-permute-done((bf16[8,8,1024]{2,1,0:T(8,128)(2,1)S(1)}, bf16[8,8,1024]{2,1,0:T(8,128)(2,1)S(1)}, u32[]{:S(2)}, u32[]{:S(2)}) %collective-permute-start.8) | collective-permute-done | bytes 131104 | tf_op jit(solution)/shard_map/ppermute | solution.py:412
  15.5 1.8 %collective-permute-start.10 = (bf16[8,8,1024]{2,1,0:T(8,128)(2,1)S(1)}, bf16[8,8,1024]{2,1,0:T(8,128)(2,1)S(1)}, u32[]{:S(2)}, u32[]{:S(2)}) collective-permute-start(bf16[8,8,1024]{2,1,0:T(8,128)(2,1)S(1)} %collective-permute-done.8.rest_8_), channel_id=1, source_target_pairs={{0,4},{1,5},{2,6},{3,7},{4,0},{5,1},{6,2},{7,3},{8,12},{9,13},{10,... | collective-permute-start | bytes 393224 | tf_op jit(solution)/shard_map/ppermute | solution.py:412
  17.3 0.2 collective-permute-start.14
  17.5 1.8 %collective-permute-start.6 = (bf16[8,8,1024]{2,1,0:T(8,128)(2,1)S(1)}, bf16[8,8,1024]{2,1,0:T(8,128)(2,1)S(1)}, u32[]{:S(2)}, u32[]{:S(2)}) collective-permute-start(bf16[8,8,1024]{2,1,0:T(8,128)(2,1)S(1)} %collective-permute-done.4.rest_4_), channel_id=1, source_target_pairs={{0,4},{1,5},{2,6},{3,7},{4,0},{5,1},{6,2},{7,3},{8,12},{9,13},{10,... | collective-permute-start | bytes 393224 | tf_op jit(solution)/shard_map/ppermute | solution.py:412
  19.4 0.0 collective-permute-done.2.rest_2_
  19.4 0.0 collective-permute-start.13
  19.4 0.0 collective-permute-done.1.rest_1_
  19.4 0.5 collective-permute-start.5
  19.9 2.0 %collective-permute-done.10.rest_10_ = bf16[8,8,1024]{2,1,0:T(8,128)(2,1)S(1)} collective-permute-done((bf16[8,8,1024]{2,1,0:T(8,128)(2,1)S(1)}, bf16[8,8,1024]{2,1,0:T(8,128)(2,1)S(1)}, u32[]{:S(2)}, u32[]{:S(2)}) %collective-permute-start.10) | collective-permute-done | bytes 131104 | tf_op jit(solution)/shard_map/ppermute | solution.py:412
  21.9 0.0 collective-permute-start.9
  21.9 1.7 %collective-permute-done.14.rest_14_ = bf16[8,8,1024]{2,1,0:T(8,128)(2,1)S(1)} collective-permute-done((bf16[8,8,1024]{2,1,0:T(8,128)(2,1)S(1)}, bf16[8,8,1024]{2,1,0:T(8,128)(2,1)S(1)}, u32[]{:S(2)}, u32[]{:S(2)}) %collective-permute-start.14) | collective-permute-done | bytes 131104 | tf_op jit(solution)/shard_map/ppermute | solution.py:412
  23.5 0.0 collective-permute-start.3
  23.5 1.4 %collective-permute-done.6.rest_6_ = bf16[8,8,1024]{2,1,0:T(8,128)(2,1)S(1)} collective-permute-done((bf16[8,8,1024]{2,1,0:T(8,128)(2,1)S(1)}, bf16[8,8,1024]{2,1,0:T(8,128)(2,1)S(1)}, u32[]{:S(2)}, u32[]{:S(2)}) %collective-permute-start.6) | collective-permute-done | bytes 131104 | tf_op jit(solution)/shard_map/ppermute | solution.py:412
  24.9 0.0 collective-permute-done.13.rest_13_
  24.9 0.5 collective-permute-start.15
  25.4 0.0 collective-permute-done.5.rest_5_
  25.4 0.1 collective-permute-start.7
  25.5 0.1 pad_add_fusion.place_ref
  25.6 0.2 reshape.9.rest_0_
  26.4 0.8 fusion.4.rest_4_
  27.2 1.3 %collective-permute-start = (bf16[64,1024]{1,0:T(8,128)(2,1)S(1)}, bf16[64,1024]{1,0:T(8,128)(2,1)S(1)}, u32[]{:S(2)}, u32[]{:S(2)}) collective-permute-start(bf16[64,1024]{1,0:T(8,128)(2,1)S(1)} %reshape.9.rest_0_), channel_id=1, source_target_pairs={{0,2},{1,3},{2,0},{3,1},{4,6},{5,7},{6,4},{7,5},{8,10},{9,11},{10,... | collective-permute-start | bytes 393224 | tf_op jit(solution)/shard_map/ppermute | solution.py:412
  28.5 0.8 collective-permute-start.18
  29.3 0.0 collective-permute-done.11.rest_11_
  29.3 0.0 collective-permute-done.15.rest_15_
  29.3 0.0 collective-permute-done.7.rest_7_
  29.3 0.0 copy-start.2
  29.4 0.6 copy-done.2
  30.0 6.5 %mean_first.1.rest_2_ = bf16[64,1024]{1,0:T(8,128)(2,1)S(1)} custom-call(s32[3]{0:T(128)S(1)} %pad_add_fusion.place_ref, s32[64]{0:T(128)S(1)} %bitcast.21, s32[1]{0:T(128)S(6)} %copy.17.count_ref, s32[1024,512]{1,0:T(8,128)} %adj_ref.3, bf16[8,8,1024]{2,1,0:T(8,128)(2,1)S(1)} %reshape_reshape.3.rest_0_, ...), custom_call_target="tpu_custom_call" | custom-call | flops 2013265920 | bytes 2097152 | tf_op jit(solution)/shard_map/mean_first/pallas_call | solution.py:253
  36.5 0.0 copy-start.3
  36.5 1.3 %collective-permute-start.16 = (bf16[64,1024]{1,0:T(8,128)(2,1)S(1)}, bf16[64,1024]{1,0:T(8,128)(2,1)S(1)}, u32[]{:S(2)}, u32[]{:S(2)}) collective-permute-start(bf16[64,1024]{1,0:T(8,128)(2,1)S(1)} %mean_first.1.rest_2_), channel_id=1, source_target_pairs={{0,2},{1,3},{2,0},{3,1},{4,6},{5,7},{6,4},{7,5},{8,10},{9,11},{10,... | collective-permute-start | bytes 393224 | tf_op jit(solution)/shard_map/ppermute | solution.py:412
  37.8 0.5 collective-permute-start.19
  38.3 0.8 collective-permute-done.17.rest_5_
  39.1 0.2 collective-permute-done.19.rest_7_
  39.3 2.6 %collective-permute-done.16.rest_3_ = bf16[64,1024]{1,0:T(8,128)(2,1)S(1)} collective-permute-done((bf16[64,1024]{1,0:T(8,128)(2,1)S(1)}, bf16[64,1024]{1,0:T(8,128)(2,1)S(1)}, u32[]{:S(2)}, u32[]{:S(2)}) %collective-permute-start.16) | collective-permute-done | bytes 131104 | tf_op jit(solution)/shard_map/ppermute | solution.py:412
  41.9 1.4 %hidden.1 = (bf16[1024,256]{1,0:T(8,128)(2,1)S(1)}, bf16[64,1408]{1,0:T(8,128)(2,1)S(1)}, bf16[96,256]{1,0:T(8,128)(2,1)S(1)}) custom-call(s32[3]{0:T(128)S(1)} %pad_add_fusion.place_ref, bf16[64,1024]{1,0:T(8,128)(2,1)S(1)} %reshape.9.rest_0_, bf16[64,1024]{1,0:T(8,128)(2,1)S(1)} %collective-permute-done.rest_1_, bf16[64,1024]{1,0:T(8,128)(2,1)S(1)} %mean_first.1.rest_2_, ...), custom_call_target="tpu_custom_call" | custom-call | tf_op jit(solution)/shard_map/hidden/pallas_call | solution.py:456
  43.3 1.5 %collective-permute-start.23 = (bf16[8,8,1408]{2,1,0:T(8,128)(2,1)S(1)}, bf16[8,8,1408]{2,1,0:T(8,128)(2,1)S(1)}, u32[]{:S(2)}, u32[]{:S(2)}) collective-permute-start(bf16[8,8,1408]{2,1,0:T(8,128)(2,1)S(1)} %bitcast.15), channel_id=1, source_target_pairs={{0,8},{1,9},{2,10},{3,11},{4,12},{5,13},{6,14},{7,15},{8,0},{9,1},... | collective-permute-start | bytes 540680 | tf_op jit(solution)/shard_map/ppermute | solution.py:412
  44.8 3.4 %collective-permute-start.27 = (bf16[8,8,1408]{2,1,0:T(8,128)(2,1)S(1)}, bf16[8,8,1408]{2,1,0:T(8,128)(2,1)S(1)}, u32[]{:S(2)}, u32[]{:S(2)}) collective-permute-start(bf16[8,8,1408]{2,1,0:T(8,128)(2,1)S(1)} %bitcast.16), channel_id=1, source_target_pairs={{0,16},{1,17},{2,18},{3,19},{4,20},{5,21},{6,22},{7,23},{8,24},{9,... | collective-permute-start | bytes 540680 | tf_op jit(solution)/shard_map/ppermute | solution.py:412
  48.2 1.5 %collective-permute-start.21 = (bf16[8,8,1408]{2,1,0:T(8,128)(2,1)S(1)}, bf16[8,8,1408]{2,1,0:T(8,128)(2,1)S(1)}, u32[]{:S(2)}, u32[]{:S(2)}) collective-permute-start(bf16[8,8,1408]{2,1,0:T(8,128)(2,1)S(1)} %bitcast.17), channel_id=1, source_target_pairs={{0,4},{1,5},{2,6},{3,7},{4,0},{5,1},{6,2},{7,3},{8,12},{9,13},{10,... | collective-permute-start | bytes 540680 | tf_op jit(solution)/shard_map/ppermute | solution.py:412
  49.7 0.0 collective-permute-start.31
  50.4 2.9 %prepare.1 = (s16[1024,512]{1,0:T(8,128)(2,1)S(1)}, s32[1024,128]{1,0:T(8,128)S(1)}, f32[1024,128]{1,0:T(8,128)S(1)}) custom-call(s32[3]{0:T(128)S(1)} %pad_add_fusion.place_ref, s32[64]{0:T(128)S(1)} %bitcast.12, s32[1]{0:T(128)S(6)} %copy.18.count_ref, s32[1024,512]{1,0:T(8,128)} %adj_ref.2), custom_call_target="tpu_custom_call" | custom-call | flops 134217728 | bytes 2097152 | tf_op jit(solution)/shard_map/prepare/pallas_call | solution.py:276
  53.3 8.1 %collective-permute-done.27.rest_8_ = bf16[8,8,1408]{2,1,0:T(8,128)(2,1)S(1)} collective-permute-done((bf16[8,8,1408]{2,1,0:T(8,128)(2,1)S(1)}, bf16[8,8,1408]{2,1,0:T(8,128)(2,1)S(1)}, u32[]{:S(2)}, u32[]{:S(2)}) %collective-permute-start.27) | collective-permute-done | bytes 180256 | tf_op jit(solution)/shard_map/ppermute | solution.py:412
  61.3 1.5 %collective-permute-start.25 = (bf16[8,8,1408]{2,1,0:T(8,128)(2,1)S(1)}, bf16[8,8,1408]{2,1,0:T(8,128)(2,1)S(1)}, u32[]{:S(2)}, u32[]{:S(2)}) collective-permute-start(bf16[8,8,1408]{2,1,0:T(8,128)(2,1)S(1)} %collective-permute-done.23.rest_4_), channel_id=1, source_target_pairs={{0,4},{1,5},{2,6},{3,7},{4,0},{5,1},{6,2},{7,3},{8,12},{9,13},{10,... | collective-permute-start | bytes 540680 | tf_op jit(solution)/shard_map/ppermute | solution.py:412
  62.9 0.6 collective-permute-start.29
  63.4 0.2 collective-permute-start.22
  63.6 5.1 %collective-permute-done.25.rest_6_ = bf16[8,8,1408]{2,1,0:T(8,128)(2,1)S(1)} collective-permute-done((bf16[8,8,1408]{2,1,0:T(8,128)(2,1)S(1)}, bf16[8,8,1408]{2,1,0:T(8,128)(2,1)S(1)}, u32[]{:S(2)}, u32[]{:S(2)}) %collective-permute-start.25) | collective-permute-done | bytes 180256 | tf_op jit(solution)/shard_map/ppermute | solution.py:412
  68.7 2.7 %collective-permute-done.29.rest_10_ = bf16[8,8,1408]{2,1,0:T(8,128)(2,1)S(1)} collective-permute-done((bf16[8,8,1408]{2,1,0:T(8,128)(2,1)S(1)}, bf16[8,8,1408]{2,1,0:T(8,128)(2,1)S(1)}, u32[]{:S(2)}, u32[]{:S(2)}) %collective-permute-start.29) | collective-permute-done | bytes 180256 | tf_op jit(solution)/shard_map/ppermute | solution.py:412
  71.4 1.5 %collective-permute-start.34 = (bf16[8,8,1408]{2,1,0:T(8,128)(2,1)S(1)}, bf16[8,8,1408]{2,1,0:T(8,128)(2,1)S(1)}, u32[]{:S(2)}, u32[]{:S(2)}) collective-permute-start(bf16[8,8,1408]{2,1,0:T(8,128)(2,1)S(1)} %collective-permute-done.31.rest_12_), channel_id=1, source_target_pairs={{0,4},{1,5},{2,6},{3,7},{4,0},{5,1},{6,2},{7,3},{8,12},{9,13},{10,... | collective-permute-start | bytes 540680 | tf_op jit(solution)/shard_map/ppermute | solution.py:412
  72.9 0.2 collective-permute-start.26
  73.2 0.3 collective-permute-start.30
  73.5 2.2 %own_rows.1.own_ref = f32[128,1024]{1,0:T(8,128)S(1)} custom-call(s32[1,1024]{1,0:T(1,128)S(1)} %bitcast.11, bf16[96,256]{1,0:T(8,128)(2,1)S(1)} %get-tuple-element.15.weight_ref, bf16[1024,256]{1,0:T(8,128)(2,1)S(1)} %get-tuple-element.16.rest_0_, bf16[1024,256]{1,0:T(8,128)(2,1)S(1)} %collective-permute-done.33.rest_1_), custom_call_target="tpu_custom_call" | custom-call | flops 3221225472 | bytes 352256 | tf_op jit(solution)/shard_map/own_rows/pallas_call | solution.py:490
  75.7 2.7 %collective-permute-done.34.rest_0_ = bf16[8,8,1408]{2,1,0:T(8,128)(2,1)S(1)} collective-permute-done((bf16[8,8,1408]{2,1,0:T(8,128)(2,1)S(1)}, bf16[8,8,1408]{2,1,0:T(8,128)(2,1)S(1)}, u32[]{:S(2)}, u32[]{:S(2)}) %collective-permute-start.34) | collective-permute-done | bytes 180256 | tf_op jit(solution)/shard_map/ppermute | solution.py:412
  78.4 5.8 %mean_main.1.main_ref = f32[1024,128]{1,0:T(8,128)S(1)} custom-call(s32[3]{0:T(128)S(1)} %pad_add_fusion.place_ref, s32[64]{0:T(128)S(1)} %bitcast.13, s16[1024,512]{1,0:T(8,128)(2,1)S(1)} %get-tuple-element.13.short_ref, bf16[8,8,1408]{2,1,0:T(8,128)(2,1)S(1)} %bitcast.20, bf16[8,8,1408]{2,1,0:T(8,128)(2,1)S(1)} %collective-permute-done.20.rest_1_, ...), custom_call_target="tpu_custom_call" | custom-call | flops 2013265920 | bytes 2097152 | tf_op jit(solution)/shard_map/mean_main/pallas_call | solution.py:299
  84.2 2.4 %mean_late.1 = bf16[86,1024]{1,0:T(8,128)(2,1)S(1)} custom-call(s32[3]{0:T(128)S(1)} %pad_add_fusion.place_ref, s32[64]{0:T(128)S(1)} %bitcast.14, s32[1024,128]{1,0:T(8,128)S(1)} %get-tuple-element.11.words_ref, f32[1024,128]{1,0:T(8,128)S(1)} %get-tuple-element.12.degree_ref, f32[1024,128]{1,0:T(8,128)S(1)} %mean_main.1.main_ref, ...), custom_call_target="tpu_custom_call" | custom-call | flops 503316480 | bytes 524288 | tf_op jit(solution)/shard_map/mean_late/pallas_call | solution.py:310
  86.6 1.6 %collective-permute-start.36 = (bf16[86,1024]{1,0:T(8,128)(2,1)S(1)}, bf16[86,1024]{1,0:T(8,128)(2,1)S(1)}, u32[]{:S(2)}, u32[]{:S(2)}) collective-permute-start(bf16[86,1024]{1,0:T(8,128)(2,1)S(1)} %mean_late.1), channel_id=1, source_target_pairs={{0,2},{1,3},{2,0},{3,1},{4,6},{5,7},{6,4},{7,5},{8,10},{9,11},{10,... | collective-permute-start | bytes 528392 | tf_op jit(solution)/shard_map/ppermute | solution.py:412
  88.2 5.5 %collective-permute-done.36 = bf16[86,1024]{1,0:T(8,128)(2,1)S(1)} collective-permute-done((bf16[86,1024]{1,0:T(8,128)(2,1)S(1)}, bf16[86,1024]{1,0:T(8,128)(2,1)S(1)}, u32[]{:S(2)}, u32[]{:S(2)}) %collective-permute-start.36) | collective-permute-done | bytes 176160 | tf_op jit(solution)/shard_map/ppermute | solution.py:412
  93.7 0.9 convert_bitcast_fusion
  (33 shorter events, 0.1 us)
Async XLA Ops:
  0.0 1.0 %copy-start = (bf16[2048,64]{0,1:T(8,128)(2,1)S(1)}, bf16[2048,64]{0,1:T(8,128)(2,1)}, u32[]{:S(2)}) copy-start(bf16[2048,64]{0,1:T(8,128)(2,1)} %param.12) | copy-start | bytes 786436
  1.4 14.1 %collective-permute-start.8 = (bf16[8,8,1024]{2,1,0:T(8,128)(2,1)S(1)}, bf16[8,8,1024]{2,1,0:T(8,128)(2,1)S(1)}, u32[]{:S(2)}, u32[]{:S(2)}) collective-permute-start(bf16[8,8,1024]{2,1,0:T(8,128)(2,1)S(1)} %reshape_reshape.3.rest_0_), channel_id=1, source_target_pairs={{0,16},{1,17},{2,18},{3,19},{4,20},{5,21},{6,22},{7,23},{8,24},{9,... | collective-permute-start | bytes 393224 | tf_op jit(solution)/shard_map/ppermute | solution.py:412
  5.5 11.8 %collective-permute-start.12 = (bf16[8,8,1024]{2,1,0:T(8,128)(2,1)S(1)}, bf16[8,8,1024]{2,1,0:T(8,128)(2,1)S(1)}, u32[]{:S(2)}, u32[]{:S(2)}) collective-permute-start(bf16[8,8,1024]{2,1,0:T(8,128)(2,1)S(1)} %reshape_reshape.3.rest_0_), channel_id=1, source_target_pairs={{0,24},{1,25},{2,26},{3,27},{4,28},{5,29},{6,30},{7,31},{8,16},{9,... | collective-permute-start | bytes 393224 | tf_op jit(solution)/shard_map/ppermute | solution.py:412
  6.8 10.7 %collective-permute-start.4 = (bf16[8,8,1024]{2,1,0:T(8,128)(2,1)S(1)}, bf16[8,8,1024]{2,1,0:T(8,128)(2,1)S(1)}, u32[]{:S(2)}, u32[]{:S(2)}) collective-permute-start(bf16[8,8,1024]{2,1,0:T(8,128)(2,1)S(1)} %reshape_reshape.3.rest_0_), channel_id=1, source_target_pairs={{0,8},{1,9},{2,10},{3,11},{4,12},{5,13},{6,14},{7,15},{8,0},{9,1},... | collective-permute-start | bytes 393224 | tf_op jit(solution)/shard_map/ppermute | solution.py:412
  7.1 12.3 %collective-permute-start.2 = (bf16[8,8,1024]{2,1,0:T(8,128)(2,1)S(1)}, bf16[8,8,1024]{2,1,0:T(8,128)(2,1)S(1)}, u32[]{:S(2)}, u32[]{:S(2)}) collective-permute-start(bf16[8,8,1024]{2,1,0:T(8,128)(2,1)S(1)} %reshape_reshape.3.rest_0_), channel_id=1, source_target_pairs={{0,4},{1,5},{2,6},{3,7},{4,0},{5,1},{6,2},{7,3},{8,12},{9,13},{10,... | collective-permute-start | bytes 393224 | tf_op jit(solution)/shard_map/ppermute | solution.py:412
  8.6 10.8 %collective-permute-start.1 = (bf16[8,8,1024]{2,1,0:T(8,128)(2,1)S(1)}, bf16[8,8,1024]{2,1,0:T(8,128)(2,1)S(1)}, u32[]{:S(2)}, u32[]{:S(2)}) collective-permute-start(bf16[8,8,1024]{2,1,0:T(8,128)(2,1)S(1)} %reshape_reshape.3.rest_0_), channel_id=1, source_target_pairs={{0,1},{1,0},{2,3},{3,2},{4,5},{5,4},{6,7},{7,6},{8,9},{9,8},{10,11... | collective-permute-start | bytes 393224 | tf_op jit(solution)/shard_map/ppermute | solution.py:412
  15.5 6.4 %collective-permute-start.10 = (bf16[8,8,1024]{2,1,0:T(8,128)(2,1)S(1)}, bf16[8,8,1024]{2,1,0:T(8,128)(2,1)S(1)}, u32[]{:S(2)}, u32[]{:S(2)}) collective-permute-start(bf16[8,8,1024]{2,1,0:T(8,128)(2,1)S(1)} %collective-permute-done.8.rest_8_), channel_id=1, source_target_pairs={{0,4},{1,5},{2,6},{3,7},{4,0},{5,1},{6,2},{7,3},{8,12},{9,13},{10,... | collective-permute-start | bytes 393224 | tf_op jit(solution)/shard_map/ppermute | solution.py:412
  17.3 6.2 %collective-permute-start.14 = (bf16[8,8,1024]{2,1,0:T(8,128)(2,1)S(1)}, bf16[8,8,1024]{2,1,0:T(8,128)(2,1)S(1)}, u32[]{:S(2)}, u32[]{:S(2)}) collective-permute-start(bf16[8,8,1024]{2,1,0:T(8,128)(2,1)S(1)} %collective-permute-done.12.rest_12_), channel_id=1, source_target_pairs={{0,4},{1,5},{2,6},{3,7},{4,0},{5,1},{6,2},{7,3},{8,12},{9,13},{10,... | collective-permute-start | bytes 393224 | tf_op jit(solution)/shard_map/ppermute | solution.py:412
  17.5 7.4 %collective-permute-start.6 = (bf16[8,8,1024]{2,1,0:T(8,128)(2,1)S(1)}, bf16[8,8,1024]{2,1,0:T(8,128)(2,1)S(1)}, u32[]{:S(2)}, u32[]{:S(2)}) collective-permute-start(bf16[8,8,1024]{2,1,0:T(8,128)(2,1)S(1)} %collective-permute-done.4.rest_4_), channel_id=1, source_target_pairs={{0,4},{1,5},{2,6},{3,7},{4,0},{5,1},{6,2},{7,3},{8,12},{9,13},{10,... | collective-permute-start | bytes 393224 | tf_op jit(solution)/shard_map/ppermute | solution.py:412
  19.4 5.6 %collective-permute-start.13 = (bf16[8,8,1024]{2,1,0:T(8,128)(2,1)S(1)}, bf16[8,8,1024]{2,1,0:T(8,128)(2,1)S(1)}, u32[]{:S(2)}, u32[]{:S(2)}) collective-permute-start(bf16[8,8,1024]{2,1,0:T(8,128)(2,1)S(1)} %collective-permute-done.12.rest_12_), channel_id=1, source_target_pairs={{0,1},{1,0},{2,3},{3,2},{4,5},{5,4},{6,7},{7,6},{8,9},{9,8},{10,11... | collective-permute-start | bytes 393224 | tf_op jit(solution)/shard_map/ppermute | solution.py:412
  19.4 6.1 %collective-permute-start.5 = (bf16[8,8,1024]{2,1,0:T(8,128)(2,1)S(1)}, bf16[8,8,1024]{2,1,0:T(8,128)(2,1)S(1)}, u32[]{:S(2)}, u32[]{:S(2)}) collective-permute-start(bf16[8,8,1024]{2,1,0:T(8,128)(2,1)S(1)} %collective-permute-done.4.rest_4_), channel_id=1, source_target_pairs={{0,1},{1,0},{2,3},{3,2},{4,5},{5,4},{6,7},{7,6},{8,9},{9,8},{10,11... | collective-permute-start | bytes 393224 | tf_op jit(solution)/shard_map/ppermute | solution.py:412
  21.9 5.4 %collective-permute-start.9 = (bf16[8,8,1024]{2,1,0:T(8,128)(2,1)S(1)}, bf16[8,8,1024]{2,1,0:T(8,128)(2,1)S(1)}, u32[]{:S(2)}, u32[]{:S(2)}) collective-permute-start(bf16[8,8,1024]{2,1,0:T(8,128)(2,1)S(1)} %collective-permute-done.8.rest_8_), channel_id=1, source_target_pairs={{0,1},{1,0},{2,3},{3,2},{4,5},{5,4},{6,7},{7,6},{8,9},{9,8},{10,11... | collective-permute-start | bytes 393224 | tf_op jit(solution)/shard_map/ppermute | solution.py:412
  23.5 5.0 %collective-permute-start.3 = (bf16[8,8,1024]{2,1,0:T(8,128)(2,1)S(1)}, bf16[8,8,1024]{2,1,0:T(8,128)(2,1)S(1)}, u32[]{:S(2)}, u32[]{:S(2)}) collective-permute-start(bf16[8,8,1024]{2,1,0:T(8,128)(2,1)S(1)} %collective-permute-done.2.rest_2_), channel_id=1, source_target_pairs={{0,1},{1,0},{2,3},{3,2},{4,5},{5,4},{6,7},{7,6},{8,9},{9,8},{10,11... | collective-permute-start | bytes 393224 | tf_op jit(solution)/shard_map/ppermute | solution.py:412
  24.9 4.4 %collective-permute-start.11 = (bf16[8,8,1024]{2,1,0:T(8,128)(2,1)S(1)}, bf16[8,8,1024]{2,1,0:T(8,128)(2,1)S(1)}, u32[]{:S(2)}, u32[]{:S(2)}) collective-permute-start(bf16[8,8,1024]{2,1,0:T(8,128)(2,1)S(1)} %collective-permute-done.10.rest_10_), channel_id=1, source_target_pairs={{0,1},{1,0},{2,3},{3,2},{4,5},{5,4},{6,7},{7,6},{8,9},{9,8},{10,11... | collective-permute-start | bytes 393224 | tf_op jit(solution)/shard_map/ppermute | solution.py:412
  24.9 4.4 %collective-permute-start.15 = (bf16[8,8,1024]{2,1,0:T(8,128)(2,1)S(1)}, bf16[8,8,1024]{2,1,0:T(8,128)(2,1)S(1)}, u32[]{:S(2)}, u32[]{:S(2)}) collective-permute-start(bf16[8,8,1024]{2,1,0:T(8,128)(2,1)S(1)} %collective-permute-done.14.rest_14_), channel_id=1, source_target_pairs={{0,1},{1,0},{2,3},{3,2},{4,5},{5,4},{6,7},{7,6},{8,9},{9,8},{10,11... | collective-permute-start | bytes 393224 | tf_op jit(solution)/shard_map/ppermute | solution.py:412
  25.4 3.9 %collective-permute-start.7 = (bf16[8,8,1024]{2,1,0:T(8,128)(2,1)S(1)}, bf16[8,8,1024]{2,1,0:T(8,128)(2,1)S(1)}, u32[]{:S(2)}, u32[]{:S(2)}) collective-permute-start(bf16[8,8,1024]{2,1,0:T(8,128)(2,1)S(1)} %collective-permute-done.6.rest_6_), channel_id=1, source_target_pairs={{0,1},{1,0},{2,3},{3,2},{4,5},{5,4},{6,7},{7,6},{8,9},{9,8},{10,11... | collective-permute-start | bytes 393224 | tf_op jit(solution)/shard_map/ppermute | solution.py:412
  27.2 11.9 %collective-permute-start = (bf16[64,1024]{1,0:T(8,128)(2,1)S(1)}, bf16[64,1024]{1,0:T(8,128)(2,1)S(1)}, u32[]{:S(2)}, u32[]{:S(2)}) collective-permute-start(bf16[64,1024]{1,0:T(8,128)(2,1)S(1)} %reshape.9.rest_0_), channel_id=1, source_target_pairs={{0,2},{1,3},{2,0},{3,1},{4,6},{5,7},{6,4},{7,5},{8,10},{9,11},{10,... | collective-permute-start | bytes 393224 | tf_op jit(solution)/shard_map/ppermute | solution.py:412
  28.5 9.3 %collective-permute-start.18 = (bf16[320,128]{1,0:T(8,128)(2,1)S(1)}, bf16[320,128]{1,0:T(8,128)(2,1)S(1)}, u32[]{:S(2)}, u32[]{:S(2)}) collective-permute-start(bf16[320,128]{1,0:T(8,128)(2,1)S(1)} %fusion.4.rest_4_), channel_id=1, source_target_pairs={{0,2},{1,3},{2,0},{3,1},{4,6},{5,7},{6,4},{7,5},{8,10},{9,11},{10,... | collective-permute-start | bytes 245768 | tf_op jit(solution)/shard_map/ppermute | solution.py:412
  29.3 0.7 copy-start.2
  30.0 20.4 %copy-start.1 = (s32[1,64]{1,0:T(1,128)S(1)}, s32[1,64]{1,0:T(1,128)}, u32[]{:S(2)}) copy-start(s32[1,64]{1,0:T(1,128)} %param.20) | copy-start | bytes 772
  36.5 27.1 %copy-start.3 = (s32[1024]{0:T(1024)S(1)}, s32[1024]{0:T(1024)}, u32[]{:S(2)}) copy-start(s32[1024]{0:T(1024)} %param.23) | copy-start | bytes 12292
  36.5 5.3 %collective-permute-start.16 = (bf16[64,1024]{1,0:T(8,128)(2,1)S(1)}, bf16[64,1024]{1,0:T(8,128)(2,1)S(1)}, u32[]{:S(2)}, u32[]{:S(2)}) collective-permute-start(bf16[64,1024]{1,0:T(8,128)(2,1)S(1)} %mean_first.1.rest_2_), channel_id=1, source_target_pairs={{0,2},{1,3},{2,0},{3,1},{4,6},{5,7},{6,4},{7,5},{8,10},{9,11},{10,... | collective-permute-start | bytes 393224 | tf_op jit(solution)/shard_map/ppermute | solution.py:412
  37.8 1.3 %collective-permute-start.17 = (bf16[320,128]{1,0:T(8,128)(2,1)S(1)}, bf16[320,128]{1,0:T(8,128)(2,1)S(1)}, u32[]{:S(2)}, u32[]{:S(2)}) collective-permute-start(bf16[320,128]{1,0:T(8,128)(2,1)S(1)} %fusion.4.rest_4_), channel_id=1, source_target_pairs={{0,1},{1,0},{2,3},{3,2},{4,5},{5,4},{6,7},{7,6},{8,9},{9,8},{10,11... | collective-permute-start | bytes 245768 | tf_op jit(solution)/shard_map/ppermute | solution.py:412
  37.8 1.4 %collective-permute-start.19 = (bf16[320,128]{1,0:T(8,128)(2,1)S(1)}, bf16[320,128]{1,0:T(8,128)(2,1)S(1)}, u32[]{:S(2)}, u32[]{:S(2)}) collective-permute-start(bf16[320,128]{1,0:T(8,128)(2,1)S(1)} %collective-permute-done.18.rest_6_), channel_id=1, source_target_pairs={{0,1},{1,0},{2,3},{3,2},{4,5},{5,4},{6,7},{7,6},{8,9},{9,8},{10,11... | collective-permute-start | bytes 245768 | tf_op jit(solution)/shard_map/ppermute | solution.py:412
  43.3 6.5 %collective-permute-start.23 = (bf16[8,8,1408]{2,1,0:T(8,128)(2,1)S(1)}, bf16[8,8,1408]{2,1,0:T(8,128)(2,1)S(1)}, u32[]{:S(2)}, u32[]{:S(2)}) collective-permute-start(bf16[8,8,1408]{2,1,0:T(8,128)(2,1)S(1)} %bitcast.15), channel_id=1, source_target_pairs={{0,8},{1,9},{2,10},{3,11},{4,12},{5,13},{6,14},{7,15},{8,0},{9,1},... | collective-permute-start | bytes 540680 | tf_op jit(solution)/shard_map/ppermute | solution.py:412
  44.8 28.3 %collective-permute-start.33 = (bf16[1024,256]{1,0:T(8,128)(2,1)S(1)}, bf16[1024,256]{1,0:T(8,128)(2,1)S(1)}, u32[]{:S(2)}, u32[]{:S(2)}) collective-permute-start(bf16[1024,256]{1,0:T(8,128)(2,1)S(1)} %get-tuple-element.16.rest_0_), channel_id=1, source_target_pairs={{0,1},{1,0},{2,3},{3,2},{4,5},{5,4},{6,7},{7,6},{8,9},{9,8},{10,11... | collective-permute-start | bytes 1572872 | tf_op jit(solution)/shard_map/ppermute | solution.py:412
  44.8 16.5 %collective-permute-start.27 = (bf16[8,8,1408]{2,1,0:T(8,128)(2,1)S(1)}, bf16[8,8,1408]{2,1,0:T(8,128)(2,1)S(1)}, u32[]{:S(2)}, u32[]{:S(2)}) collective-permute-start(bf16[8,8,1408]{2,1,0:T(8,128)(2,1)S(1)} %bitcast.16), channel_id=1, source_target_pairs={{0,16},{1,17},{2,18},{3,19},{4,20},{5,21},{6,22},{7,23},{8,24},{9,... | collective-permute-start | bytes 540680 | tf_op jit(solution)/shard_map/ppermute | solution.py:412
  48.2 14.6 %collective-permute-start.21 = (bf16[8,8,1408]{2,1,0:T(8,128)(2,1)S(1)}, bf16[8,8,1408]{2,1,0:T(8,128)(2,1)S(1)}, u32[]{:S(2)}, u32[]{:S(2)}) collective-permute-start(bf16[8,8,1408]{2,1,0:T(8,128)(2,1)S(1)} %bitcast.17), channel_id=1, source_target_pairs={{0,4},{1,5},{2,6},{3,7},{4,0},{5,1},{6,2},{7,3},{8,12},{9,13},{10,... | collective-permute-start | bytes 540680 | tf_op jit(solution)/shard_map/ppermute | solution.py:412
  49.7 13.1 %collective-permute-start.31 = (bf16[8,8,1408]{2,1,0:T(8,128)(2,1)S(1)}, bf16[8,8,1408]{2,1,0:T(8,128)(2,1)S(1)}, u32[]{:S(2)}, u32[]{:S(2)}) collective-permute-start(bf16[8,8,1408]{2,1,0:T(8,128)(2,1)S(1)} %bitcast.18), channel_id=1, source_target_pairs={{0,24},{1,25},{2,26},{3,27},{4,28},{5,29},{6,30},{7,31},{8,16},{9,... | collective-permute-start | bytes 540680 | tf_op jit(solution)/shard_map/ppermute | solution.py:412
  49.7 13.7 %collective-permute-start.20 = (bf16[8,8,1408]{2,1,0:T(8,128)(2,1)S(1)}, bf16[8,8,1408]{2,1,0:T(8,128)(2,1)S(1)}, u32[]{:S(2)}, u32[]{:S(2)}) collective-permute-start(bf16[8,8,1408]{2,1,0:T(8,128)(2,1)S(1)} %bitcast.19), channel_id=1, source_target_pairs={{0,1},{1,0},{2,3},{3,2},{4,5},{5,4},{6,7},{7,6},{8,9},{9,8},{10,11... | collective-permute-start | bytes 540680 | tf_op jit(solution)/shard_map/ppermute | solution.py:412
  61.3 7.4 %collective-permute-start.25 = (bf16[8,8,1408]{2,1,0:T(8,128)(2,1)S(1)}, bf16[8,8,1408]{2,1,0:T(8,128)(2,1)S(1)}, u32[]{:S(2)}, u32[]{:S(2)}) collective-permute-start(bf16[8,8,1408]{2,1,0:T(8,128)(2,1)S(1)} %collective-permute-done.23.rest_4_), channel_id=1, source_target_pairs={{0,4},{1,5},{2,6},{3,7},{4,0},{5,1},{6,2},{7,3},{8,12},{9,13},{10,... | collective-permute-start | bytes 540680 | tf_op jit(solution)/shard_map/ppermute | solution.py:412
  62.8 10.1 %collective-permute-start.24 = (bf16[8,8,1408]{2,1,0:T(8,128)(2,1)S(1)}, bf16[8,8,1408]{2,1,0:T(8,128)(2,1)S(1)}, u32[]{:S(2)}, u32[]{:S(2)}) collective-permute-start(bf16[8,8,1408]{2,1,0:T(8,128)(2,1)S(1)} %collective-permute-done.23.rest_4_), channel_id=1, source_target_pairs={{0,1},{1,0},{2,3},{3,2},{4,5},{5,4},{6,7},{7,6},{8,9},{9,8},{10,11... | collective-permute-start | bytes 540680 | tf_op jit(solution)/shard_map/ppermute | solution.py:412
  62.9 8.6 %collective-permute-start.29 = (bf16[8,8,1408]{2,1,0:T(8,128)(2,1)S(1)}, bf16[8,8,1408]{2,1,0:T(8,128)(2,1)S(1)}, u32[]{:S(2)}, u32[]{:S(2)}) collective-permute-start(bf16[8,8,1408]{2,1,0:T(8,128)(2,1)S(1)} %collective-permute-done.27.rest_8_), channel_id=1, source_target_pairs={{0,4},{1,5},{2,6},{3,7},{4,0},{5,1},{6,2},{7,3},{8,12},{9,13},{10,... | collective-permute-start | bytes 540680 | tf_op jit(solution)/shard_map/ppermute | solution.py:412
  63.4 8.0 %collective-permute-start.22 = (bf16[8,8,1408]{2,1,0:T(8,128)(2,1)S(1)}, bf16[8,8,1408]{2,1,0:T(8,128)(2,1)S(1)}, u32[]{:S(2)}, u32[]{:S(2)}) collective-permute-start(bf16[8,8,1408]{2,1,0:T(8,128)(2,1)S(1)} %collective-permute-done.21.rest_2_), channel_id=1, source_target_pairs={{0,1},{1,0},{2,3},{3,2},{4,5},{5,4},{6,7},{7,6},{8,9},{9,8},{10,11... | collective-permute-start | bytes 540680 | tf_op jit(solution)/shard_map/ppermute | solution.py:412
  68.7 9.6 %collective-permute-start.28 = (bf16[8,8,1408]{2,1,0:T(8,128)(2,1)S(1)}, bf16[8,8,1408]{2,1,0:T(8,128)(2,1)S(1)}, u32[]{:S(2)}, u32[]{:S(2)}) collective-permute-start(bf16[8,8,1408]{2,1,0:T(8,128)(2,1)S(1)} %collective-permute-done.27.rest_8_), channel_id=1, source_target_pairs={{0,1},{1,0},{2,3},{3,2},{4,5},{5,4},{6,7},{7,6},{8,9},{9,8},{10,11... | collective-permute-start | bytes 540680 | tf_op jit(solution)/shard_map/ppermute | solution.py:412
  71.4 7.0 %collective-permute-start.32 = (bf16[8,8,1408]{2,1,0:T(8,128)(2,1)S(1)}, bf16[8,8,1408]{2,1,0:T(8,128)(2,1)S(1)}, u32[]{:S(2)}, u32[]{:S(2)}) collective-permute-start(bf16[8,8,1408]{2,1,0:T(8,128)(2,1)S(1)} %collective-permute-done.31.rest_12_), channel_id=1, source_target_pairs={{0,1},{1,0},{2,3},{3,2},{4,5},{5,4},{6,7},{7,6},{8,9},{9,8},{10,11... | collective-permute-start | bytes 540680 | tf_op jit(solution)/shard_map/ppermute | solution.py:412
  71.4 7.0 %collective-permute-start.34 = (bf16[8,8,1408]{2,1,0:T(8,128)(2,1)S(1)}, bf16[8,8,1408]{2,1,0:T(8,128)(2,1)S(1)}, u32[]{:S(2)}, u32[]{:S(2)}) collective-permute-start(bf16[8,8,1408]{2,1,0:T(8,128)(2,1)S(1)} %collective-permute-done.31.rest_12_), channel_id=1, source_target_pairs={{0,4},{1,5},{2,6},{3,7},{4,0},{5,1},{6,2},{7,3},{8,12},{9,13},{10,... | collective-permute-start | bytes 540680 | tf_op jit(solution)/shard_map/ppermute | solution.py:412
  72.9 5.5 %collective-permute-start.26 = (bf16[8,8,1408]{2,1,0:T(8,128)(2,1)S(1)}, bf16[8,8,1408]{2,1,0:T(8,128)(2,1)S(1)}, u32[]{:S(2)}, u32[]{:S(2)}) collective-permute-start(bf16[8,8,1408]{2,1,0:T(8,128)(2,1)S(1)} %collective-permute-done.25.rest_6_), channel_id=1, source_target_pairs={{0,1},{1,0},{2,3},{3,2},{4,5},{5,4},{6,7},{7,6},{8,9},{9,8},{10,11... | collective-permute-start | bytes 540680 | tf_op jit(solution)/shard_map/ppermute | solution.py:412
  73.2 5.2 %collective-permute-start.30 = (bf16[8,8,1408]{2,1,0:T(8,128)(2,1)S(1)}, bf16[8,8,1408]{2,1,0:T(8,128)(2,1)S(1)}, u32[]{:S(2)}, u32[]{:S(2)}) collective-permute-start(bf16[8,8,1408]{2,1,0:T(8,128)(2,1)S(1)} %collective-permute-done.29.rest_10_), channel_id=1, source_target_pairs={{0,1},{1,0},{2,3},{3,2},{4,5},{5,4},{6,7},{7,6},{8,9},{9,8},{10,11... | collective-permute-start | bytes 540680 | tf_op jit(solution)/shard_map/ppermute | solution.py:412
  78.4 5.8 %collective-permute-start.35 = (bf16[8,8,1408]{2,1,0:T(8,128)(2,1)S(1)}, bf16[8,8,1408]{2,1,0:T(8,128)(2,1)S(1)}, u32[]{:S(2)}, u32[]{:S(2)}) collective-permute-start(bf16[8,8,1408]{2,1,0:T(8,128)(2,1)S(1)} %collective-permute-done.34.rest_0_), channel_id=1, source_target_pairs={{0,1},{1,0},{2,3},{3,2},{4,5},{5,4},{6,7},{7,6},{8,9},{9,8},{10,11... | collective-permute-start | bytes 540680 | tf_op jit(solution)/shard_map/ppermute | solution.py:412
  86.6 7.0 %collective-permute-start.36 = (bf16[86,1024]{1,0:T(8,128)(2,1)S(1)}, bf16[86,1024]{1,0:T(8,128)(2,1)S(1)}, u32[]{:S(2)}, u32[]{:S(2)}) collective-permute-start(bf16[86,1024]{1,0:T(8,128)(2,1)S(1)} %mean_late.1), channel_id=1, source_target_pairs={{0,2},{1,3},{2,0},{3,1},{4,6},{5,7},{6,4},{7,5},{8,10},{9,11},{10,... | collective-permute-start | bytes 528392 | tf_op jit(solution)/shard_map/ppermute | solution.py:412
